TPU v7x, 32 devices: a whole 2x2x4 slice. The times are simulated.
32 devices in a mesh: rep: 1, r: 4 (over z), s: 8 (over x, y, core).
Axes of the slice: x: 2, y: 2, z: 4, core: 2. Of those that a mesh axis runs over, the one named last changes fastest.
Arguments:
- x: bfloat16 [32, 4096, 512], P(('rep', 'r', 's'))
- dy: bfloat16 [32, 4096, 512], P(('rep', 'r', 's'))
- w_gate: bfloat16 [2, 512, 1664], P(None, 's')
- w_up: bfloat16 [2, 512, 1664], P(None, 's')
- w_down: bfloat16 [2, 1664, 512], P(None, 's')
- m_w_gate: float32 [2, 512, 1664], P(None, 's')
- m_w_up: float32 [2, 512, 1664], P(None, 's')
- m_w_down: float32 [2, 1664, 512], P(None, 's')
- v_w_gate: float32 [2, 512, 1664], P(None, 's')
- v_w_up: float32 [2, 512, 1664], P(None, 's')
- v_w_down: float32 [2, 1664, 512], P(None, 's')
Outputs:
- output 1: bfloat16 [2, 512, 1664], P('rep', 's')
- output 2: bfloat16 [2, 512, 1664], P('rep', 's')
- output 3: bfloat16 [2, 1664, 512], P('rep', 's')
- output 4: float32 [2, 512, 1664], P('rep', 's')
- output 5: float32 [2, 512, 1664], P('rep', 's')
- output 6: float32 [2, 1664, 512], P('rep', 's')
- output 7: float32 [2, 512, 1664], P('rep', 's')
- output 8: float32 [2, 512, 1664], P('rep', 's')
- output 9: float32 [2, 1664, 512], P('rep', 's')
All inputs are finite; a program needn't handle non-finite values.
Results may differ from a plain program's by a relative error of at most 0.02.
Values are sent between devices in bfloat16 or wider.
A program may use at most 2 GiB of HBM per device.

v0:
```python
import jax
import jax.numpy as jnp
from jax import lax
from jax.sharding import PartitionSpec as P

NAMES = ("w_gate", "w_up", "w_down")


def matmul(a, w):
    return jnp.dot(a, w, preferred_element_type=jnp.float32).astype(jnp.bfloat16)


def normed(h):
    wide = h.astype(jnp.float32)
    scale = lax.rsqrt(jnp.mean(wide**2, -1, keepdims=True) + 1e-6)
    return (wide * scale).astype(jnp.bfloat16)


def layer(h, w):
    a = normed(h)
    gate = jnp.dot(a, w["w_gate"], preferred_element_type=jnp.float32)
    up = jnp.dot(a, w["w_up"], preferred_element_type=jnp.float32)
    return h + matmul((jax.nn.silu(gate) * up).astype(jnp.bfloat16), w["w_down"])


def adamw(w, m, v, g):
    m = 0.9 * m + 0.1 * g
    v = 0.95 * v + 0.05 * g * g
    step = m * lax.rsqrt(v + 1e-8) + 0.1 * w
    return (w - 0.02 * step).astype(jnp.bfloat16), m, v


def solution(mesh):
    def fetched(weights, number):
        return {name: lax.all_gather(w[number], "s", axis=0, tiled=True) for name, w in zip(NAMES, weights, strict=True)}

    def summed(term):
        return lax.psum(lax.psum_scatter(term, "s", scatter_dimension=0, tiled=True), "r")

    def step(x, dy, *arrays):
        weights, m, v = (arrays[i : i + 3] for i in (0, 3, 6))
        layers = weights[0].shape[0]
        h, kept = x[0], []
        for number in range(layers):
            kept.append(h)
            h = layer(h, fetched(weights, number))
        by_h, mine = dy[0], [None] * layers
        for number in reversed(range(layers)):
            _, back = jax.vjp(lambda w, h: layer(h, w), fetched(weights, number), kept[number])
            by_w, by_h = back(by_h)
            mine[number] = [summed(by_w[name]) for name in NAMES]
        gradients = [jnp.stack([mine[number][i] for number in range(layers)]).astype(jnp.float32) for i in range(3)]
        new = [adamw(w.astype(jnp.float32), m, v, g) for w, m, v, g in zip(weights, m, v, gradients, strict=True)]
        return tuple(one[which] for which in range(3) for one in new)

    states, cut = P(("rep", "r", "s"), None, None), P(None, "s", None)
    return jax.shard_map(
        step,
        mesh=mesh,
        in_specs=(states, states) + (cut,) * 9,
        out_specs=(P("rep", "s", None),) * 9,
        check_vma=False,
    )
```

profile of v0, /device:TPU:0, one launch (start us, length us, event | category | flops | bytes accessed | tf_op | source)
XLA Modules:
  0.0 589.0 jit_solution(9968304584406144153)
XLA Ops:
  7.2 1.8 fusion.87
  9.1 0.0 all-gather.15.cloned.1.call-start
  9.1 1.8 fusion.86
  11.0 0.0 all-gather.17.cloned.1.call-start
  11.0 1.8 fusion.85
  12.9 0.0 all-gather.21.cloned.1.call-start
  12.9 0.5 all-gather.21.cloned.1.call-update
  13.5 0.5 all-gather.23.cloned.1.call-update
  14.1 0.5 all-gather.19.cloned.1.call-update
  14.6 6.4 %copy.20 = bf16[1,4096,512]{1,2,0:T(8,128)(2,1)} copy(bf16[1,4096,512]{2,1,0:T(8,128)(2,1)} %param.11) | data formatting | bytes 8388608 | tf_op args[0]
  21.0 3.1 fusion.15
  24.1 6.4 %copy.21 = bf16[1,4096,512]{1,2,0:T(8,128)(2,1)} copy(bf16[1,4096,512]{2,1,0:T(8,128)(2,1)} %param.12) | data formatting | bytes 8388608 | tf_op args[1]
  30.6 8.5 %all-gather.13.cloned.1.call-done = bf16[1,512,1664]{2,1,0:T(8,128)(2,1)} async-done(((bf16[1,64,1664]{2,1,0:T(8,128)(2,1)}), bf16[1,512,1664]{2,1,0:T(8,128)(2,1)}) %all-gather.13.cloned.1.call-update) | async-done | bytes 1703952 | tf_op jit(solution)/shard_map/all_gather | solution.py:35
  39.1 15.1 %fusion.47 = f32[4096,1664]{1,0:T(8,128)} fusion(bf16[1,4096,512]{1,2,0:T(8,128)(2,1)} %copy.20, f32[4096]{0:T(1024)S(1)} %add_rsqrt_fusion, bf16[1,512,1664]{2,1,0:T(8,128)(2,1)} %all-gather.13.cloned.1.call-done), kind=kOutput, calls=%fused_computation.57 | convolution fusion | flops 6985613312 | bytes 33177600 | tf_op jit(solution)/shard_map/dot_general | solution.py:21
  54.2 13.2 %all-gather.15.cloned.1.call-done = bf16[1,512,1664]{2,1,0:T(8,128)(2,1)} async-done(((bf16[1,64,1664]{2,1,0:T(8,128)(2,1)}), bf16[1,512,1664]{2,1,0:T(8,128)(2,1)}) %all-gather.15.cloned.1.call-update) | async-done | bytes 1703952 | tf_op jit(solution)/shard_map/all_gather | solution.py:35
  67.4 27.6 %multiply_convert_fusion.1 = (bf16[4096,1664]{1,0:T(8,128)(2,1)}, f32[4096,1664]{1,0:T(8,128)}) fusion(f32[4096,1664]{1,0:T(8,128)} %fusion.47, bf16[1,512,1664]{2,1,0:T(8,128)(2,1)} %all-gather.15.cloned.1.call-done, bf16[1,4096,512]{1,2,0:T(8,128)(2,1)} %copy.20, f32[4096]{0:T(1024)S(1)} %add_rsqrt_fusion), kind=kOutput, calls=%fused_computation.17 | convolution fusion | flops 7026507776 | bytes 74072064 | tf_op jit(solution)/shard_map/dot_general | solution.py:22
  95.1 0.7 all-gather.17.cloned.1.call-done
  95.8 14.2 %fusion.19 = (f32[4096]{0:T(1024)S(1)}, bf16[4096,512]{0,1:T(8,128)(2,1)}) fusion(bf16[4096,1664]{1,0:T(8,128)(2,1)} %get-tuple-element.30, bf16[1,1664,512]{2,1,0:T(8,128)(2,1)} %all-gather.17.cloned.1.call-done, bf16[1,4096,512]{1,2,0:T(8,128)(2,1)} %copy.20), kind=kOutput, calls=%fused_computation.37 | convolution fusion | flops 6989803520 | bytes 23740416 | tf_op jit(solution)/shard_map/dot_general | solution.py:10
  110.0 0.6 copy-done.9
  110.6 13.4 %all-gather.21.cloned.1.call-done = bf16[1,1664,512]{2,1,0:T(8,128)(2,1)} async-done(((bf16[1,208,512]{2,1,0:T(8,128)(2,1)}), bf16[1,1664,512]{2,1,0:T(8,128)(2,1)}) %all-gather.21.cloned.1.call-update) | async-done | bytes 1703952 | tf_op jit(solution)/shard_map/all_gather | solution.py:35
  124.0 12.9 %convolution_convert_fusion.1 = bf16[4096,1664]{1,0:T(8,128)(2,1)} fusion(bf16[1,4096,512]{2,1,0:T(8,128)(2,1)} %param.12, bf16[1,1664,512]{2,1,0:T(8,128)(2,1)} %all-gather.21.cloned.1.call-done), kind=kOutput, calls=%fused_computation.23 | convolution fusion | flops 6986137600 | bytes 19529728 | tf_op jit(solution)/shard_map/transpose(jvp())/dot_general | solution.py:10
  136.9 15.3 %all-gather.23.cloned.1.call-done = bf16[1,512,1664]{2,1,0:T(8,128)(2,1)} async-done(((bf16[1,64,1664]{2,1,0:T(8,128)(2,1)}), bf16[1,512,1664]{2,1,0:T(8,128)(2,1)}) %all-gather.23.cloned.1.call-update) | async-done | bytes 1703952 | tf_op jit(solution)/shard_map/all_gather | solution.py:35
  152.2 15.0 %fusion.39 = f32[4096,1664]{1,0:T(8,128)} fusion(bf16[4096,512]{0,1:T(8,128)(2,1)} %get-tuple-element.33, f32[4096]{0:T(1024)S(1)} %fusion.73, bf16[1,512,1664]{2,1,0:T(8,128)(2,1)} %all-gather.23.cloned.1.call-done), kind=kOutput, calls=%fused_computation.54 | convolution fusion | flops 6985613312 | bytes 33177600 | tf_op jit(solution)/shard_map/jvp()/dot_general | solution.py:22
  167.2 13.2 %all-gather.19.cloned.1.call-done = bf16[1,512,1664]{2,1,0:T(8,128)(2,1)} async-done(((bf16[1,64,1664]{2,1,0:T(8,128)(2,1)}), bf16[1,512,1664]{2,1,0:T(8,128)(2,1)}) %all-gather.19.cloned.1.call-update) | async-done | bytes 1703952 | tf_op jit(solution)/shard_map/all_gather | solution.py:35
  180.4 36.8 %fusion.2 = (bf16[4096,1664]{1,0:T(8,128)(2,1)}, f32[4096,1664]{1,0:T(8,128)}) fusion(f32[4096,1664]{1,0:T(8,128)} %fusion.39, bf16[4096,1664]{1,0:T(8,128)(2,1)} %convolution_convert_fusion.1, bf16[1,512,1664]{2,1,0:T(8,128)(2,1)} %all-gather.19.cloned.1.call-done, bf16[4096,512]{0,1:T(8,128)(2,1)} %get-tuple-element.33, f32[4096]{0:T(1024)S(1)} %fusion.73), kind=kOutput, calls=%fused_computation.8 | convolution fusion | flops 7067402240 | bytes 87703552 | tf_op jit(solution)/shard_map/jvp()/dot_general | solution.py:21
  217.2 14.5 %convolution_convert_fusion.4 = bf16[512,1664]{1,0:T(8,128)(2,1)} fusion(bf16[4096,1664]{1,0:T(8,128)(2,1)} %get-tuple-element.34, bf16[4096,512]{0,1:T(8,128)(2,1)} %get-tuple-element.33, f32[4096]{0:T(1024)S(1)} %fusion.73), kind=kOutput, calls=%fused_computation.49 | convolution fusion | flops 6985613312 | bytes 19546112 | tf_op jit(solution)/shard_map/transpose(jvp())/dot_general | solution.py:21
  231.8 0.0 reduce-scatter.7.cloned.1.call-start
  231.8 19.3 %fusion.22 = bf16[4096,512]{0,1:T(8,128)(2,1)} fusion(bf16[4096,1664]{1,0:T(8,128)(2,1)} %convolution_convert_fusion.1, bf16[1,512,1664]{2,1,0:T(8,128)(2,1)S(1)} %copy-done.14, f32[4096,1664]{1,0:T(8,128)} %get-tuple-element.35), kind=kOutput, calls=%fused_computation.40 | convolution fusion | flops 7022313472 | bytes 46792704 | tf_op jit(solution)/shard_map/transpose(jvp())/dot_general | solution.py:22
  251.1 13.7 %fusion.21 = (f32[4096]{0:T(1024)S(1)}, bf16[4096,512]{0,1:T(8,128)(2,1)S(1)}) fusion(bf16[4096,512]{0,1:T(8,128)(2,1)} %get-tuple-element.33, bf16[4096,512]{0,1:T(8,128)(2,1)} %fusion.22, bf16[4096,1664]{1,0:T(8,128)(2,1)} %get-tuple-element.34, bf16[1,512,1664]{2,1,0:T(8,128)(2,1)} %all-gather.19.cloned.1.call-done), kind=kOutput, calls=%fused_computation.39 | convolution fusion | flops 6989803520 | bytes 27934720 | tf_op jit(solution)/shard_map/transpose(jvp())/dot_general | solution.py:21
  264.9 3.1 fusion.26
  268.1 11.2 %convolution_convert_fusion = bf16[4096,1664]{1,0:T(8,128)(2,1)} fusion(bf16[4096,512]{0,1:T(8,128)(2,1)S(1)} %fusion.26, bf16[1,1664,512]{2,1,0:T(8,128)(2,1)S(1)} %copy-done.13), kind=kOutput, calls=%fused_computation.22 | convolution fusion | flops 6986137600 | bytes 19529728 | tf_op jit(solution)/shard_map/transpose(jvp())/dot_general | solution.py:10
  279.3 25.7 %fusion.34 = bf16[512,1664]{1,0:T(8,128)(2,1)} fusion(f32[4096,1664]{1,0:T(8,128)} %fusion.47, f32[4096,1664]{1,0:T(8,128)} %get-tuple-element.31, bf16[4096,1664]{1,0:T(8,128)(2,1)} %convolution_convert_fusion, bf16[1,4096,512]{1,2,0:T(8,128)(2,1)S(1)} %copy-done, f32[4096]{0:T(1024)S(1)} %copy-done.12), kind=kOutput, calls=%fused_computation.53 | convolution fusion | flops 7061438464 | bytes 74072064 | tf_op jit(solution)/shard_map/transpose(jvp())/dot_general | solution.py:21
  305.0 0.0 reduce-scatter.13.cloned.1.call-start
  305.1 20.2 %fusion.33 = bf16[512,1664]{1,0:T(8,128)(2,1)} fusion(bf16[4096,1664]{1,0:T(8,128)(2,1)} %convolution_convert_fusion.1, bf16[4096,512]{0,1:T(8,128)(2,1)} %get-tuple-element.33, f32[4096]{0:T(1024)S(1)} %fusion.73, f32[4096,1664]{1,0:T(8,128)} %get-tuple-element.35), kind=kOutput, calls=%fused_computation.51 | convolution fusion | flops 7027359744 | bytes 46809088 | tf_op jit(solution)/shard_map/transpose(jvp())/dot_general | solution.py:22
  325.3 0.0 reduce-scatter.11.cloned.1.call-start
  325.3 19.8 %fusion.29 = bf16[512,1664]{1,0:T(8,128)(2,1)} fusion(bf16[4096,1664]{1,0:T(8,128)(2,1)} %convolution_convert_fusion, f32[4096,1664]{1,0:T(8,128)} %fusion.47, bf16[1,4096,512]{1,2,0:T(8,128)(2,1)} %copy.20, f32[4096]{0:T(1024)S(1)} %copy-done.12), kind=kOutput, calls=%fused_computation.48 | convolution fusion | flops 7027359744 | bytes 46809088 | tf_op jit(solution)/shard_map/transpose(jvp())/dot_general | solution.py:22
  345.1 0.0 reduce-scatter.17.cloned.1.call-start
  345.2 22.9 %fusion.30 = bf16[1664,512]{1,0:T(8,128)(2,1)} fusion(bf16[1,4096,512]{2,1,0:T(8,128)(2,1)} %param.12, f32[4096,1664]{1,0:T(8,128)} %fusion.39, f32[4096,1664]{1,0:T(8,128)} %get-tuple-element.35), kind=kOutput, calls=%fused_computation.50 | convolution fusion | flops 7021068288 | bytes 60424192 | tf_op jit(solution)/shard_map/transpose(jvp())/dot_general | solution.py:10
  368.2 0.0 reduce-scatter.15.cloned.1.call-start
  368.3 14.1 %convolution_convert_fusion.5 = bf16[1664,512]{1,0:T(8,128)(2,1)} fusion(bf16[4096,1664]{1,0:T(8,128)(2,1)} %get-tuple-element.30, bf16[4096,512]{0,1:T(8,128)(2,1)} %copy-done.3), kind=kOutput, calls=%fused_computation.52 | convolution fusion | flops 6980173824 | bytes 19529728 | tf_op jit(solution)/shard_map/transpose(jvp())/dot_general | solution.py:10
  382.4 0.0 all-reduce.3.cloned.1.call-start
  382.5 3.5 reduce-scatter.13.cloned.1.call-done
  386.0 41.9 %reduce-scatter.11.cloned.1.call-done = bf16[64,1664]{1,0:T(8,128)(2,1)} async-done(((bf16[512,1664]{1,0:T(8,128)(2,1)}), bf16[64,1664]{1,0:T(8,128)(2,1)}) %reduce-scatter.11.cloned.1.call-update) | async-done | bytes 213008 | tf_op jit(solution)/shard_map/reduce_scatter | solution.py:38
  428.0 42.1 %reduce-scatter.17.cloned.1.call-done = bf16[208,512]{1,0:T(8,128)(2,1)} async-done(((bf16[1664,512]{1,0:T(8,128)(2,1)}), bf16[208,512]{1,0:T(8,128)(2,1)}) %reduce-scatter.17.cloned.1.call-update) | async-done | bytes 213008 | tf_op jit(solution)/shard_map/reduce_scatter | solution.py:38
  470.1 42.0 %reduce-scatter.15.cloned.1.call-done = bf16[208,512]{1,0:T(8,128)(2,1)} async-done(((bf16[1664,512]{1,0:T(8,128)(2,1)}), bf16[208,512]{1,0:T(8,128)(2,1)}) %reduce-scatter.15.cloned.1.call-update) | async-done | bytes 213008 | tf_op jit(solution)/shard_map/reduce_scatter | solution.py:38
  512.0 62.6 %all-reduce.3.cloned.1.call-done = (bf16[1,64,1664]{2,1,0:T(8,128)(2,1)}, bf16[1,64,1664]{2,1,0:T(8,128)(2,1)}, bf16[1,64,1664]{2,1,0:T(8,128)(2,1)}, bf16[1,64,...) async-done(((bf16[1,64,1664]{2,1,0:T(8,128)(2,1)}, bf16[1,64,1664]{2,1,0:T(8,128)(2,1)}, bf16[1,64,1664]{2,1,0:T(8,128)(2,1)}, ...) | async-done | bytes 1277968 | tf_op jit(solution)/shard_map/psum | solution.py:38
  574.6 2.6 fusion.68
  577.2 4.7 fusion.60
  (48 shorter events, 0.5 us)
Async XLA Ops:
  7.2 31.9 %all-gather.13.cloned.1.call-start = ((), (), s32[]{:S(2)}) async-start(), calls=%async_computation.12 | async-start | bytes 1916928 | tf_op jit(solution)/shard_map/all_gather | solution.py:35
  9.1 58.4 %all-gather.15.cloned.1.call-start = ((), (), s32[]{:S(2)}) async-start(), calls=%async_computation.13 | async-start | bytes 1916928 | tf_op jit(solution)/shard_map/all_gather | solution.py:35
  11.0 84.8 %all-gather.17.cloned.1.call-start = ((), (), s32[]{:S(2)}) async-start(), calls=%async_computation.14 | async-start | bytes 1916928 | tf_op jit(solution)/shard_map/all_gather | solution.py:35
  12.9 111.2 %all-gather.21.cloned.1.call-start = ((), (), s32[]{:S(2)}) async-start(), calls=%async_computation.16 | async-start | bytes 1916928 | tf_op jit(solution)/shard_map/all_gather | solution.py:35
  13.4 138.8 %all-gather.23.cloned.1.call-start = ((), (), s32[]{:S(2)}) async-start(), calls=%async_computation.17 | async-start | bytes 1916928 | tf_op jit(solution)/shard_map/all_gather | solution.py:35
  14.0 166.4 %all-gather.19.cloned.1.call-start = ((), (), s32[]{:S(2)}) async-start(), calls=%async_computation.15 | async-start | bytes 1916928 | tf_op jit(solution)/shard_map/all_gather | solution.py:35
  14.6 367.9 %reduce-scatter.9.cloned.1.call-start = ((), (), s32[]{:S(2)}) async-start(), calls=%async_computation.7 | async-start | bytes 1916928 | tf_op jit(solution)/shard_map/reduce_scatter | solution.py:38
  24.1 43.3 %copy-start.11 = (f32[4096]{0:T(1024)}, f32[4096]{0:T(1024)S(1)}, u32[]{:S(2)}) copy-start(f32[4096]{0:T(1024)S(1)} %add_rsqrt_fusion) | copy-start | bytes 49156
  110.0 0.6 copy-start.9
  217.2 14.6 %copy-start.14 = (bf16[1,512,1664]{2,1,0:T(8,128)(2,1)S(1)}, bf16[1,512,1664]{2,1,0:T(8,128)(2,1)}, u32[]{:S(2)}) copy-start(bf16[1,512,1664]{2,1,0:T(8,128)(2,1)} %all-gather.23.cloned.1.call-done) | copy-start | bytes 5111812
  231.8 150.8 %reduce-scatter.7.cloned.1.call-start = ((), (), s32[]{:S(2)}) async-start(), calls=%async_computation.6 | async-start | bytes 1916928 | tf_op jit(solution)/shard_map/reduce_scatter | solution.py:38
  251.1 13.8 %copy-start.10 = (f32[4096]{0:T(1024)S(1)}, f32[4096]{0:T(1024)}, u32[]{:S(2)}) copy-start(f32[4096]{0:T(1024)} %copy-done.9) | copy-start | bytes 49156
  251.1 13.8 %copy-start.1 = (bf16[1,4096,512]{1,2,0:T(8,128)(2,1)S(1)}, bf16[1,4096,512]{1,2,0:T(8,128)(2,1)}, u32[]{:S(2)}) copy-start(bf16[1,4096,512]{1,2,0:T(8,128)(2,1)} %copy.21) | copy-start | bytes 12582916
  251.1 13.8 %copy-start.2 = (bf16[4096,512]{0,1:T(8,128)(2,1)S(1)}, bf16[4096,512]{0,1:T(8,128)(2,1)}, u32[]{:S(2)}) copy-start(bf16[4096,512]{0,1:T(8,128)(2,1)} %get-tuple-element.33) | copy-start | bytes 12582916
  264.9 3.2 copy-start.13
  268.1 11.2 %copy-start.3 = (bf16[4096,512]{0,1:T(8,128)(2,1)}, bf16[4096,512]{0,1:T(8,128)(2,1)S(1)}, u32[]{:S(2)}) copy-start(bf16[4096,512]{0,1:T(8,128)(2,1)S(1)} %fusion.26) | copy-start | bytes 12582916
  268.1 11.2 %copy-start = (bf16[1,4096,512]{1,2,0:T(8,128)(2,1)S(1)}, bf16[1,4096,512]{1,2,0:T(8,128)(2,1)}, u32[]{:S(2)}) copy-start(bf16[1,4096,512]{1,2,0:T(8,128)(2,1)} %copy.20) | copy-start | bytes 12582916
  268.1 11.2 %copy-start.12 = (f32[4096]{0:T(1024)S(1)}, f32[4096]{0:T(1024)}, u32[]{:S(2)}) copy-start(f32[4096]{0:T(1024)} %copy-done.11) | copy-start | bytes 49156
  305.0 81.0 %reduce-scatter.13.cloned.1.call-start = ((), (), s32[]{:S(2)}) async-start(), calls=%async_computation.9 | async-start | bytes 1916928 | tf_op jit(solution)/shard_map/reduce_scatter | solution.py:38
  325.3 102.7 %reduce-scatter.11.cloned.1.call-start = ((), (), s32[]{:S(2)}) async-start(), calls=%async_computation.8 | async-start | bytes 1916928 | tf_op jit(solution)/shard_map/reduce_scatter | solution.py:38
  345.1 124.9 %reduce-scatter.17.cloned.1.call-start = ((), (), s32[]{:S(2)}) async-start(), calls=%async_computation.11 | async-start | bytes 1916928 | tf_op jit(solution)/shard_map/reduce_scatter | solution.py:38
  368.2 206.5 %copy-start.4 = (bf16[2,208,512]{2,1,0:T(8,128)(2,1)S(1)}, bf16[2,208,512]{2,1,0:T(8,128)(2,1)}, u32[]{:S(2)}) copy-start(bf16[2,208,512]{2,1,0:T(8,128)(2,1)} %param.15) | copy-start | bytes 1277956
  368.2 206.4 %copy-start.7 = (f32[2,208,512]{2,1,0:T(8,128)S(1)}, f32[2,208,512]{2,1,0:T(8,128)}, u32[]{:S(2)}) copy-start(f32[2,208,512]{2,1,0:T(8,128)} %param.21) | copy-start | bytes 2555908
  368.2 206.4 %copy-start.8 = (f32[2,208,512]{2,1,0:T(8,128)S(1)}, f32[2,208,512]{2,1,0:T(8,128)}, u32[]{:S(2)}) copy-start(f32[2,208,512]{2,1,0:T(8,128)} %param.18) | copy-start | bytes 2555908
  368.2 209.0 %copy-start.5 = (bf16[2,64,1664]{2,1,0:T(8,128)(2,1)S(1)}, bf16[2,64,1664]{2,1,0:T(8,128)(2,1)}, u32[]{:S(2)}) copy-start(bf16[2,64,1664]{2,1,0:T(8,128)(2,1)} %param.13) | copy-start | bytes 1277956
  368.2 209.0 %copy-start.6 = (bf16[2,64,1664]{2,1,0:T(8,128)(2,1)S(1)}, bf16[2,64,1664]{2,1,0:T(8,128)(2,1)}, u32[]{:S(2)}) copy-start(bf16[2,64,1664]{2,1,0:T(8,128)(2,1)} %param.14) | copy-start | bytes 1277956
  368.2 143.8 %reduce-scatter.15.cloned.1.call-start = ((), (), s32[]{:S(2)}) async-start(), calls=%async_computation.10 | async-start | bytes 1916928 | tf_op jit(solution)/shard_map/reduce_scatter | solution.py:38
  382.4 192.2 %all-reduce.3.cloned.1.call-start = ((), (), s32[]{:S(2)}) async-start(), calls=%async_computation.18 | async-start | bytes 2555904 | tf_op jit(solution)/shard_map/psum | solution.py:38
Sparse Core Ops, SparseCore 0:
  10.4 28.6 all-gather.12
  41.5 25.8 all-gather.14
  69.9 25.8 all-gather.16
  98.1 25.8 all-gather.20
  126.3 25.8 all-gather.22
  154.5 25.8 all-gather.18
  231.9 38.7 reduce-scatter.8
  305.1 38.7 reduce-scatter.6
  347.2 38.7 reduce-scatter.12
  389.2 38.7 reduce-scatter.10
  431.3 38.7 reduce-scatter.16
  473.2 38.7 reduce-scatter.14
  514.9 59.7 all-reduce.2
where the time goes:
time: 597 us; the launch traced here: 589 us
  matrix products  283 us (47%)
  waiting for transfers between devices  258 us (43%)
  local copies, waits for them, and re-layouts  18.9 us (3%)
  between operations  14.6 us (2%)
  other arithmetic  13.6 us (2%)
    reduce_scatter x6, waiting for transfers between devices, summed(): lax.psum_scatter(term, 's', scatter_dimension=0, tiled=True)  130 us
    dot_general x5, matrix products, layer(): gate = jnp.dot(a, w['w_gate'], preferred_element_type=jnp.float32)  106 us
    dot_general x5, matrix products, layer(): up = jnp.dot(a, w['w_up'], preferred_element_type=jnp.float32)  102 us
    dot_general x5, matrix products, matmul(): jnp.dot(a, w, preferred_element_type=jnp.float32).astype(jnp.bfloat16)  75.3 us
    all_gather x6, waiting for transfers between devices, fetched(): lax.all_gather(w[number], 's', axis=0, tiled=True)  64.4 us
    psum x1, waiting for transfers between devices, summed(): lax.psum(lax.psum_scatter(term, 's', scatter_dimension=0, tiled=True), 'r')  62.6 us
    unnamed x32, local copies, waits for them, and re-layouts  13.5 us
  transfers between devices with their start and end apart: 13, of which 11 were waited for; matrix products, arithmetic and copies ran while one was open for 43% of the time, Pallas kernels for 0%

commit v1 on v0

v1 whole, which is shorter than its diff:
```python
import functools

import jax
import jax.numpy as jnp
from jax import lax
from jax.experimental import pallas as pl
from jax.experimental.pallas import tpu as pltpu
from jax.sharding import PartitionSpec as P

F32, BF16 = jnp.float32, jnp.bfloat16
D, FF, TOK = 512, 1664, 4096
TILE = 512
TILES = TOK // TILE
CHUNKS = ((0, 512), (512, 512), (1024, 512), (1536, 128))
VMEM_LIMIT = 66_000_000
ANY = pl.BlockSpec(memory_space=pl.ANY)
WHOLE = pl.BlockSpec(memory_space=pltpu.VMEM)


def dot(a, b):
    return jnp.dot(a, b, preferred_element_type=F32)


def dot_nt(a, b):
    return lax.dot_general(a, b, (((1,), (1,)), ((), ())), preferred_element_type=F32)


def norm(h):
    wide = h.astype(F32)
    scale = lax.rsqrt(jnp.mean(wide * wide, -1, keepdims=True) + 1e-6)
    return wide, scale


def gated(g):
    sig = 0.5 + 0.5 * jnp.tanh(0.5 * g)
    return sig, g * sig


def rows(n):
    return pl.BlockSpec((TILE, n), lambda i: (i, 0))


class Place:
    def __init__(self):
        s, z = lax.axis_index("s"), lax.axis_index("r")
        self.s, self.z = s, z
        self.x, self.y, self.c = s // 4, (s // 2) % 2, s % 2
        x, y, c = self.x, self.y, self.c
        self.partner = x * 4 + y * 2 + (1 - c)
        self.nx = (1 - x) * 4 + y * 2 + c
        self.ny = x * 4 + (1 - y) * 2 + c
        self.diag = (1 - x) * 4 + (1 - y) * 2 + c

    def at(self, s, z=None):
        return (0, self.z if z is None else z, s)


def copy_to(src, dst, send, recv, device):
    return pltpu.make_async_remote_copy(
        src_ref=src, dst_ref=dst, send_sem=send, recv_sem=recv, device_id=device, device_id_type=pl.DeviceIdType.MESH
    )


def signal(barrier, device):
    pl.semaphore_signal(barrier, inc=1, device_id=device, device_id_type=pl.DeviceIdType.MESH)


def gather_kernel(*refs):
    own, out = refs[:6], refs[6:12]
    send, recv, local = refs[12:15]
    p = Place()
    barrier = pltpu.get_barrier_semaphore()
    for n in (p.partner, p.nx, p.ny):
        signal(barrier, p.at(n))
    pl.semaphore_wait(barrier, 3)
    pending = []

    def go(i, k, src, slot, device):
        cp = copy_to(src, out[i].at[slot], send.at[i, k], recv.at[i, k], p.at(device))
        cp.start()
        return cp

    first = []
    for i in range(6):
        keep = pltpu.make_async_copy(own[i], out[i].at[p.s], local.at[i])
        keep.start()
        pending.append(keep)
        first.append((go(i, 0, own[i], p.s, p.nx), go(i, 1, own[i], p.s, p.ny), go(i, 2, own[i], p.s, p.partner)))
    for i in range(6):
        cx, cy, cp = first[i]
        cx.wait_recv()
        fx = go(i, 3, out[i].at[p.nx], p.nx, p.partner)
        if i % 2 == 0:
            dg = go(i, 5, out[i].at[p.nx], p.nx, p.ny)
        cy.wait_recv()
        fy = go(i, 4, out[i].at[p.ny], p.ny, p.partner)
        if i % 2 == 1:
            dg = go(i, 5, out[i].at[p.ny], p.ny, p.nx)
        first[i] = (cx, cy, cp, fx, fy, dg)
    for i in range(6):
        cx, cy, cp, fx, fy, dg = first[i]
        dg.wait_recv()
        fd = go(i, 6, out[i].at[p.diag], p.diag, p.partner)
        first[i] = (cx, cy, cp, fx, fy, dg, fd)
    for i in range(6):
        cx, cy, cp, fx, fy, dg, fd = first[i]
        for w in (cp, fx, fy, fd):
            w.wait_recv()
        for w in first[i]:
            w.wait_send()
    for keep in pending:
        keep.wait()


def gather(weights):
    own = [w[l] for l in range(2) for w in weights]
    out = pl.pallas_call(
        gather_kernel,
        out_shape=[jax.ShapeDtypeStruct((8,) + o.shape, BF16) for o in own],
        in_specs=[ANY] * 6,
        out_specs=[ANY] * 6,
        scratch_shapes=[pltpu.SemaphoreType.DMA((6, 7)), pltpu.SemaphoreType.DMA((6, 7)), pltpu.SemaphoreType.DMA((6,))],
        compiler_params=pltpu.CompilerParams(collective_id=0, has_side_effects=True),
        name="gather",
    )(*own)
    full = [o.reshape(8 * o.shape[1], o.shape[2]) for o in out]
    return full[:3], full[3:]


def forward_kernel(x_ref, wg, wu, wd, h1_ref, act_ref, a_ref):
    wide, scale = norm(x_ref[...])
    a = (wide * scale).astype(BF16)
    a_ref[...] = a
    for lo, n in CHUNKS:
        g = dot(a, wg[:, lo : lo + n])
        u = dot(a, wu[:, lo : lo + n])
        act_ref[:, lo : lo + n] = (gated(g)[1] * u).astype(BF16)
    mm = dot(act_ref[...], wd[...]).astype(BF16).astype(F32)
    h1_ref[...] = (wide + mm).astype(BF16)


def forward(x, w):
    return pl.pallas_call(
        forward_kernel,
        grid=(TILES,),
        out_shape=[
            jax.ShapeDtypeStruct((TOK, D), BF16),
            jax.ShapeDtypeStruct((TOK, FF), BF16),
            jax.ShapeDtypeStruct((TOK, D), BF16),
        ],
        in_specs=[rows(D), WHOLE, WHOLE, WHOLE],
        out_specs=[rows(D), rows(FF), rows(D)],
        compiler_params=pltpu.CompilerParams(vmem_limit_bytes=VMEM_LIMIT, dimension_semantics=("arbitrary",)),
        name="forward",
    )(x, *w)


def layer1_kernel(h_ref, dy_ref, act0_ref, wg, wu, wd, dh_ref, og, ou, od, od0, accg, accu, accd, accd0, dgs, dus):
    i = pl.program_id(0)

    @pl.when(i == 0)
    def _():
        for acc in (accg, accu, accd, accd0):
            acc[...] = jnp.zeros_like(acc)

    wide, scale = norm(h_ref[...])
    a = (wide * scale).astype(BF16)
    a_t = a.T
    dy = dy_ref[...]
    dy_t = dy.T
    for lo, n in CHUNKS:
        cut = slice(lo, lo + n)
        g = dot(a, wg[:, cut])
        u = dot(a, wu[:, cut])
        da = dot_nt(dy, wd[cut, :]).astype(BF16).astype(F32)
        sig, si = gated(g)
        act = (si * u).astype(BF16)
        du = (da * si).astype(BF16)
        dg = (da * u * (sig + si * (1.0 - sig))).astype(BF16)
        dgs[:, cut] = dg
        dus[:, cut] = du
        accd[:, cut] += dot(dy_t, act)
        accg[:, cut] += dot(a_t, dg)
        accu[:, cut] += dot(a_t, du)
    dn = (dot_nt(dgs[...], wg[...]) + dot_nt(dus[...], wu[...])).astype(BF16).astype(F32)
    inner = jnp.sum(dn * wide, -1, keepdims=True) * (scale * scale * scale * (1.0 / D))
    by_norm = (dn * scale - wide * inner).astype(BF16).astype(F32)
    dh = (dy.astype(F32) + by_norm).astype(BF16)
    dh_ref[...] = dh
    accd0[...] += dot(dh.T, act0_ref[...])

    @pl.when(i == TILES - 1)
    def _():
        og[...] = accg[...].astype(BF16)
        ou[...] = accu[...].astype(BF16)
        for acc, out in ((accd, od), (accd0, od0)):
            for h in range(2):
                t = acc[256 * h : 256 * h + 256, :].T.astype(BF16)
                for s in range(8):
                    out[s, h] = t[208 * s : 208 * s + 208]


def layer1(h1, dy, act0, w):
    up, down = jax.ShapeDtypeStruct((D, FF), BF16), jax.ShapeDtypeStruct((8, 2, 208, 256), BF16)
    return pl.pallas_call(
        layer1_kernel,
        grid=(TILES,),
        out_shape=[jax.ShapeDtypeStruct((TOK, D), BF16), up, up, down, down],
        in_specs=[rows(D), rows(D), rows(FF), WHOLE, WHOLE, WHOLE],
        out_specs=[rows(D), WHOLE, WHOLE, WHOLE, WHOLE],
        scratch_shapes=[pltpu.VMEM((D, FF), F32)] * 4 + [pltpu.VMEM((TILE, FF), BF16)] * 2,
        compiler_params=pltpu.CompilerParams(vmem_limit_bytes=VMEM_LIMIT, dimension_semantics=("arbitrary",)),
        name="layer1",
    )(h1, dy, act0, *w)


BULK = ((32, FF), (32, FF), (208, 256), (208, 256))
PIECES = BULK + tuple((32, n) for _, n in CHUNKS for _ in range(2))
NP = len(PIECES)
NBUF = 9


def schedule():
    plan = []

    def put(piece, steps):
        for stage, step in enumerate(steps):
            plan.append((min(step, LAST), stage, piece))

    put(0, (0, 2, 9, 15, 19, 22, 25, 99))
    put(1, (0, 2, 9, 15, 19, 22, 25, 99))
    put(2, (0, 4, 14, 20, 24, 27, 30, 99))
    put(3, (0, 4, 14, 20, 24, 27, 30, 99))
    put(4, (8, 10, 18, 23, 26, 29, 31, 99))
    put(5, (8, 10, 18, 23, 26, 29, 31, 99))
    put(6, (16, 18, 22, 26, 29, 31, 99, 99))
    put(7, (16, 18, 22, 26, 29, 31, 99, 99))
    put(8, (24, 26, 29, 31, 99, 99, 99, 99))
    put(9, (24, 26, 29, 31, 99, 99, 99, 99))
    put(10, (99,) * 8)
    put(11, (99,) * 8)
    return sorted(plan, key=lambda e: (e[0], e[1], e[2]))


STEPS = len(CHUNKS) * TILES
LAST = STEPS - 1


def backward0_kernel(*refs):
    a_ref, dh_ref, wg, wu, wd = refs[:5]
    bulk = refs[5:9]
    og, ou, od = refs[9:12]
    a_t, accg, accu = refs[12:15]
    chunk_g = refs[15 : 15 + 2 * len(CHUNKS)]
    at = 15 + 2 * len(CHUNKS)
    bufs = [refs[at + NBUF * k : at + NBUF * (k + 1)] for k in range(NP)]
    send, recv = refs[at + NBUF * NP :]
    terms = list(bulk) + list(chunk_g)

    j, i = pl.program_id(0), pl.program_id(1)
    step = j * TILES + i
    p = Place()
    z = p.z
    outer = (z == 0) | (z == 3)
    inward = jnp.where(z == 0, 1, 2)
    outward = jnp.where(z == 1, 0, 3)
    peer = 3 - z
    half, other = jnp.where(z == 1, 0, 1), jnp.where(z == 1, 1, 0)

    @pl.when(step == 0)
    def _():
        barrier = pltpu.get_barrier_semaphore()
        for n in (p.partner, p.nx, p.ny):
            signal(barrier, p.at(n))

        @pl.when(outer)
        def _():
            signal(barrier, p.at(p.s, inward))
            pl.semaphore_wait(barrier, 4)

        @pl.when(jnp.logical_not(outer))
        def _():
            signal(barrier, p.at(p.s, outward))
            signal(barrier, p.at(p.s, peer))
            pl.semaphore_wait(barrier, 5)

    def piece_stage(k, stage):
        g = terms[k]
        r0, s1, r1, s2, r2, zs, zr, zp, fin = bufs[k]
        x_first = k % 2 == 0
        mine, theirs = (p.x, 1 - p.x) if x_first else (p.y, 1 - p.y)
        mine_b, theirs_b = (p.y, 1 - p.y) if x_first else (p.x, 1 - p.x)
        na, nb = (p.nx, p.ny) if x_first else (p.ny, p.nx)

        def chip(first, second):
            return (first, second) if x_first else (second, first)

        def two(first, second):
            u, v = chip(first, second)
            return g[u, v, p.c].astype(F32) + r0[u, v].astype(F32)

        cps = (
            lambda: copy_to(g.at[:, :, 1 - p.c], r0, send.at[k, 0], recv.at[k, 0], p.at(p.partner)),
            lambda: copy_to(s1, r1, send.at[k, 1], recv.at[k, 1], p.at(na)),
            lambda: copy_to(s2, r2, send.at[k, 2], recv.at[k, 2], p.at(nb)),
        )
        if stage == 0:
            cps[0]().start()
        if stage == 1:
            cps[0]().wait_recv()
            for q in range(2):
                s1[q] = two(theirs, q).astype(BF16)
            cps[1]().start()
        if stage == 2:
            cps[1]().wait_recv()
            s2[...] = (two(mine, theirs_b) + r1[theirs_b].astype(F32)).astype(BF16)
            cps[2]().start()
        to_inner = lambda: copy_to(zs, zr, send.at[k, 3], recv.at[k, 3], p.at(p.s, inward))
        from_outer = lambda: copy_to(zs, zr, send.at[k, 3], recv.at[k, 3], p.at(p.s, outward))
        partial = lambda: copy_to(zs.at[other], zp, send.at[k, 3], recv.at[k, 4], p.at(p.s, peer))
        final_peer = lambda h: copy_to(fin.at[h], fin.at[h], send.at[k, 4], recv.at[k, 5], p.at(p.s, peer))
        final_out = lambda h, n: copy_to(fin.at[h], fin.at[h], send.at[k, 5 + n], recv.at[k, 6 + n], p.at(p.s, outward))
        final_in = lambda h, n: copy_to(fin.at[h], fin.at[h], send.at[k, 5 + n], recv.at[k, 6 + n], p.at(p.s, inward))
        xy_sum = lambda: two(mine, mine_b) + r1[mine_b].astype(F32) + r2[...].astype(F32)
        if stage == 3:
            cps[2]().wait_recv()

            @pl.when(outer)
            def _():
                zs[...] = xy_sum().astype(BF16)
                to_inner().start()

        if stage == 4:

            @pl.when(jnp.logical_not(outer))
            def _():
                from_outer().wait_recv()
                u, v = chip(mine, mine_b)
                total = g[u, v, p.c, other].astype(F32) + r0[u, v, other].astype(F32) + r1[mine_b, other].astype(F32)
                total += r2[other].astype(F32) + zr[other].astype(F32)
                zs[other] = total.astype(BF16)
                partial().start()

        if stage == 5:

            @pl.when(jnp.logical_not(outer))
            def _():
                partial().wait_recv()
                u, v = chip(mine, mine_b)
                total = g[u, v, p.c, half].astype(F32) + r0[u, v, half].astype(F32) + r1[mine_b, half].astype(F32)
                total += r2[half].astype(F32) + zr[half].astype(F32) + zp[...].astype(F32)
                fin[half] = total.astype(BF16)
                final_peer(half).start()
                final_out(half, 0).start()

        if stage == 6:

            @pl.when(jnp.logical_not(outer))
            def _():
                final_peer(other).wait_recv()
                final_out(other, 1).start()

        if stage == 7:

            @pl.when(outer)
            def _():
                final_in(0, 0).wait_recv()
                final_in(1, 1).wait_recv()
                to_inner().wait_send()

            @pl.when(jnp.logical_not(outer))
            def _():
                partial().wait_send()
                final_peer(half).wait_send()
                final_out(half, 0).wait_send()
                final_out(other, 1).wait_send()

            for cp in cps:
                cp().wait_send()
            if k in (0, 1):
                out = (og, ou)[k]
                for h in range(2):
                    out[1, 32 * h : 32 * h + 32, :] = fin[h]
            elif k in (2, 3):
                for h in range(2):
                    od[3 - k, :, 256 * h : 256 * h + 256] = fin[h]
            else:
                lo, n = CHUNKS[(k - 4) // 2]
                for h in range(2):
                    (og, ou)[k % 2][0, 32 * h : 32 * h + 32, lo : lo + n] = fin[h]

    tile = pl.ds(pl.multiple_of(i * TILE, TILE), TILE)

    @pl.when(j == 0)
    def _():
        a_t[i] = a_ref[...].T

    def body(n, lo, first):
        a, dh = a_ref[...], dh_ref[...]
        cut = pl.ds(lo, n)
        g = dot(a, wg[:, cut])
        u = dot(a, wu[:, cut])
        da = dot_nt(dh, wd[cut, :]).astype(BF16).astype(F32)
        sig, si = gated(g)
        du = (da * si).astype(BF16)
        dg = (da * u * (sig + si * (1.0 - sig))).astype(BF16)
        at_tile = a_t[i]
        pg, pu = dot(at_tile, dg), dot(at_tile, du)

        @pl.when(i == 0)
        def _():
            accg[:, :n] = pg
            accu[:, :n] = pu

        @pl.when(i > 0)
        def _():
            accg[:, :n] += pg
            accu[:, :n] += pu

    @pl.when(j < 3)
    def _():
        body(512, pl.multiple_of(j * 512, 512), None)

    @pl.when(j == 3)
    def _():
        body(128, 1536, None)

    for k, (lo, n) in enumerate(CHUNKS):

        @pl.when((j == k) & (i == TILES - 1))
        def _(k=k, n=n):
            for acc, out in ((accg, chunk_g[2 * k]), (accu, chunk_g[2 * k + 1])):
                for q in range(16):
                    c_, h_ = (q // 2) % 2, q % 2
                    out[q // 8, (q // 4) % 2, c_, h_] = acc[32 * q : 32 * q + 32, :n].astype(BF16)

    plan = schedule()
    for now in sorted({e[0] for e in plan}):

        @pl.when(step == now)
        def _(now=now):
            for when, stage, k in plan:
                if when == now:
                    piece_stage(k, stage)


def backward0(a0, dh1, w, bulk):
    tile2 = lambda n: pl.BlockSpec((TILE, n), lambda j, i: (i, 0))
    bufs = []
    for hr, hc in PIECES:
        bufs += [
            pltpu.VMEM((2, 2, 2, hr, hc), BF16),
            pltpu.VMEM((2, 2, hr, hc), BF16),
            pltpu.VMEM((2, 2, hr, hc), BF16),
            pltpu.VMEM((2, hr, hc), BF16),
            pltpu.VMEM((2, hr, hc), BF16),
            pltpu.VMEM((2, hr, hc), BF16),
            pltpu.VMEM((2, hr, hc), BF16),
            pltpu.VMEM((hr, hc), BF16),
            pltpu.VMEM((2, hr, hc), BF16),
        ]
    up, down = jax.ShapeDtypeStruct((2, 64, FF), BF16), jax.ShapeDtypeStruct((2, 208, D), BF16)
    bulk = [t.reshape((2, 2, 2, 2) + shape) for t, shape in zip(bulk, BULK, strict=True)]
    return pl.pallas_call(
        backward0_kernel,
        grid=(len(CHUNKS), TILES),
        out_shape=[up, up, down],
        in_specs=[tile2(D), tile2(D)] + [WHOLE] * 7,
        out_specs=[WHOLE] * 3,
        scratch_shapes=[pltpu.VMEM((TILES, D, TILE), BF16)]
        + [pltpu.VMEM((D, 512), F32)] * 2
        + [pltpu.VMEM((2, 2, 2, 2, 32, n), BF16) for _, n in CHUNKS for _ in range(2)]
        + bufs
        + [pltpu.SemaphoreType.DMA((NP, 7)), pltpu.SemaphoreType.DMA((NP, 8))],
        compiler_params=pltpu.CompilerParams(
            collective_id=1, has_side_effects=True, vmem_limit_bytes=VMEM_LIMIT, dimension_semantics=("arbitrary", "arbitrary")
        ),
        name="backward0",
    )(a0, dh1, *w, *bulk)


def adamw(w, m, v, g):
    m = 0.9 * m + 0.1 * g
    v = 0.95 * v + 0.05 * g * g
    step = m * lax.rsqrt(v + 1e-8) + 0.1 * w
    return (w - 0.02 * step).astype(BF16), m, v


def solution(mesh):
    def step(x, dy, *arrays):
        weights, m, v = (arrays[i : i + 3] for i in (0, 3, 6))
        w0, w1 = gather(weights)
        h1, act0, a0 = forward(x[0], w0)
        dh1, *bulk = layer1(h1, dy[0], act0, w1)
        gradients = backward0(a0, dh1, w0, bulk)
        new = [adamw(w.astype(F32), m, v, g.astype(F32)) for w, m, v, g in zip(weights, m, v, gradients, strict=True)]
        return tuple(one[which] for which in range(3) for one in new)

    states, cut = P(("rep", "r", "s"), None, None), P(None, "s", None)
    return jax.shard_map(
        step,
        mesh=mesh,
        in_specs=(states, states) + (cut,) * 9,
        out_specs=(P("rep", "s", None),) * 9,
        check_vma=False,
    )
```

time: 597 us -> 280 us (0.47); the launches traced: 589 us -> 280 us
  matrix products: 283 us -> 0 us
  Pallas kernels: 0 us -> 268 us
  waiting for transfers between devices: 258 us -> 0 us
  local copies, waits for them, and re-layouts: 18.9 us -> 4.85 us
  between operations: 14.6 us -> 0.75 us
  other arithmetic: 13.6 us -> 6.38 us
    dot_general x15 -> x0, matrix products: 283 us -> none  [the longest x5 106 us: layer(): gate = jnp.dot(a, w['w_gate'], preferred_element_type=jnp.float32)]
    pallas_call x0 -> x4, Pallas kernels: none -> 268 us  [the longest x1 101 us: backward0(): pl.pallas_call(backward0_kernel, grid=(len(CHUNKS), TILES), out_shape=[up...]
    reduce_scatter x6 -> x0, waiting for transfers between devices: 130 us -> none  [summed(): lax.psum_scatter(term, 's', scatter_dimension=0, tiled=True)]
    all_gather x6 -> x0, waiting for transfers between devices: 64.4 us -> none  [fetched(): lax.all_gather(w[number], 's', axis=0, tiled=True)]
    psum x1 -> x0, waiting for transfers between devices: 62.6 us -> none  [summed(): lax.psum(lax.psum_scatter(term, 's', scatter_dimension=0, tiled=True), 'r')]
    unnamed x32 -> x18, local copies, waits for them, and re-layouts: 13.5 us -> 0.87 us
  transfers between devices with their start and end apart: 13 -> 0, of which waited for: 11 -> 0; matrix products, arithmetic and copies ran while one was open for 43% -> 0% of each run, Pallas kernels for 0% -> 0%
where the time goes in v1:
time: 280 us
  Pallas kernels  268 us (96%)
  other arithmetic  6.38 us (2%)
  local copies, waits for them, and re-layouts  4.85 us (2%)
    pallas_call x1, Pallas kernels, backward0(): pl.pallas_call(backward0_kernel, grid=(len(CHUNKS), TILES), out_shape=[up...  101 us
    pallas_call x1, Pallas kernels, layer1(): pl.pallas_call(layer1_kernel, grid=(TILES,), out_shape=[jax.ShapeDtypeStr...  90.8 us
    pallas_call x1, Pallas kernels, gather(): pl.pallas_call(gather_kernel, out_shape=[jax.ShapeDtypeStruct((8,) + o.sh...  48.2 us
    pallas_call x1, Pallas kernels, forward(): pl.pallas_call(forward_kernel, grid=(TILES,), out_shape=[jax.ShapeDtypeSt...  28.7 us
    convert_element_type x3, other arithmetic, adamw(): return ((w - 0.02 * step).astype(BF16), m, v)  6.38 us

profile of v1, /device:TPU:0, one launch (start us, length us, event | category | flops | bytes accessed | tf_op | source)
XLA Modules:
  0.0 280.2 jit_solution(13217550214647690294)
XLA Ops:
  0.6 1.8 slice_bitcast_fusion
  2.5 2.2 slice_bitcast_fusion.1
  4.6 48.2 %gather.1 = (bf16[8,64,1664]{2,1,0:T(8,128)(2,1)}, bf16[8,64,1664]{2,1,0:T(8,128)(2,1)}, bf16[8,208,512]{2,1,0:T(8,128)(2,1)}, bf16[8,64,1664]{2,1,0:T(8,128)(2,...) custom-call(bf16[64,1664]{1,0:T(8,128)(2,1)} %get-tuple-element.58.refs_0_, ...), custom_call_target="tpu_custom_call" | custom-call | tf_op jit(solution)/shard_map/gather/pallas_call | solution.py:117
  52.8 28.7 %forward.1 = (bf16[4096,512]{1,0:T(8,128)(2,1)}, bf16[4096,1664]{1,0:T(8,128)(2,1)}, bf16[4096,512]{1,0:T(8,128)(2,1)}) custom-call(bf16[4096,512]{1,0:T(8,128)(2,1)} %bitcast.31, bf16[512,1664]{1,0:T(8,128)(2,1)} %bitcast.24, bf16[512,1664]{1,0:T(8,128)(2,1)} %bitcast.26, bf16[1664,512]{1,0:T(8,128)(2,1)} %bitcast.28), custom_call_target="tpu_custom_call" | custom-call | tf_op jit(solution)/shard_map/forward/pallas_call | solution.py:143
  81.5 90.8 %layer1.1 = (bf16[4096,512]{1,0:T(8,128)(2,1)}, bf16[512,1664]{1,0:T(8,128)(2,1)}, bf16[512,1664]{1,0:T(8,128)(2,1)}, bf16[8,2,208,256]{3,2,1,0:T(8,128)(2,1)}, bf16[8,2,208,256]{3,2,1,0:T(8,128)(2,1)}) custom-call(bf16[4096,512]{1,0:T(8,128)(2,1)} %get-tuple-element.30.h_ref, bf16[4096,512]{1,0:T(8,128)(2,1)} %bitcast.30, ...), custom_call_target="tpu_custom_call" | custom-call | tf_op jit(solution)/shard_map/layer1/pallas_call | solution.py:205
  172.3 0.0 copy-start.1
  172.3 100.6 %backward0.1 = (bf16[2,64,1664]{2,1,0:T(8,128)(2,1)}, bf16[2,64,1664]{2,1,0:T(8,128)(2,1)}, bf16[2,208,512]{2,1,0:T(8,128)(2,1)}) custom-call(bf16[4096,512]{1,0:T(8,128)(2,1)} %get-tuple-element.29.refs_0_, bf16[4096,512]{1,0:T(8,128)(2,1)} %get-tuple-element.35.refs_1_, bf16[512,1664]{1,0:T(8,128)(2,1)} %bitcast.25, bf16[512,1664]{1,0:T(8,128)(2,1)} %bitcast.27, ...), custom_call_target="tpu_custom_call" | custom-call | tf_op jit(solution)/shard_map/backward0/pallas_call | solution.py:464
  272.9 0.0 copy-done.1
  272.9 0.0 copy-start.2
  272.9 0.0 copy-start.3
  272.9 0.0 copy-start.4
  272.9 0.0 copy-start.8
  273.0 3.2 %fusion.2 = (bf16[2,64,1664]{2,1,0:T(8,128)(2,1)}, f32[2,64,1664]{2,1,0:T(8,128)}, f32[2,64,1664]{2,1,0:T(8,128)}) fusion(bf16[2,64,1664]{2,1,0:T(8,128)(2,1)S(1)} %copy-done.1, bf16[2,64,1664]{2,1,0:T(8,128)(2,1)} %get-tuple-element.40, f32[2,64,1664]{2,1,0:T(8,128)} %param.19, f32[2,64,1664]{2,1,0:T(8,128)} %param.16), kind=kLoop, calls=%fused_computation.14 | loop fusion | flops 3407872 | bytes 4685824 | tf_op jit(solution)/shard_map/convert_element_type | solution.py:486
  276.2 0.0 copy-done.2
  276.2 0.0 copy-done.3
  276.2 0.0 copy-done.4
  276.2 0.0 copy-done.8
  276.2 0.0 copy-start
  276.2 0.0 copy-start.5
  276.2 0.0 copy-start.6
  276.2 0.0 copy-start.7
  276.3 1.5 fusion.6
  277.8 0.0 copy-done
  277.8 0.1 copy-done.5
  277.9 0.6 copy-done.6
  278.5 0.1 copy-done.7
  278.6 1.6 fusion.10
Async XLA Ops:
  172.3 100.6 %copy-start.1 = (bf16[2,64,1664]{2,1,0:T(8,128)(2,1)S(1)}, bf16[2,64,1664]{2,1,0:T(8,128)(2,1)}, u32[]{:S(2)}) copy-start(bf16[2,64,1664]{2,1,0:T(8,128)(2,1)} %param.13) | copy-start | bytes 1277956
  272.9 3.3 %copy-start.2 = (bf16[2,64,1664]{2,1,0:T(8,128)(2,1)S(1)}, bf16[2,64,1664]{2,1,0:T(8,128)(2,1)}, u32[]{:S(2)}) copy-start(bf16[2,64,1664]{2,1,0:T(8,128)(2,1)} %param.14) | copy-start | bytes 1277956
  272.9 3.3 %copy-start.3 = (f32[2,64,1664]{2,1,0:T(8,128)S(1)}, f32[2,64,1664]{2,1,0:T(8,128)}, u32[]{:S(2)}) copy-start(f32[2,64,1664]{2,1,0:T(8,128)} %param.20) | copy-start | bytes 2555908
  272.9 3.3 %copy-start.4 = (f32[2,64,1664]{2,1,0:T(8,128)S(1)}, f32[2,64,1664]{2,1,0:T(8,128)}, u32[]{:S(2)}) copy-start(f32[2,64,1664]{2,1,0:T(8,128)} %param.17) | copy-start | bytes 2555908
  272.9 3.3 %copy-start.8 = (bf16[2,64,1664]{2,1,0:T(8,128)(2,1)S(1)}, bf16[2,64,1664]{2,1,0:T(8,128)(2,1)}, u32[]{:S(2)}) copy-start(bf16[2,64,1664]{2,1,0:T(8,128)(2,1)} %get-tuple-element.41) | copy-start | bytes 1277956
  276.2 1.6 copy-start
  276.2 1.7 copy-start.5
  276.2 2.3 copy-start.6
  276.2 2.4 copy-start.7

commit v2 on v1

v2 whole, which is shorter than its diff:
```python
import functools

import jax
import jax.numpy as jnp
from jax import lax
from jax.experimental import pallas as pl
from jax.experimental.pallas import tpu as pltpu
from jax.sharding import PartitionSpec as P

F32, BF16 = jnp.float32, jnp.bfloat16
D, FF, TOK = 512, 1664, 4096
TILE = 1024
TILES = TOK // TILE
CHUNKS = ((0, 512), (512, 512), (1024, 512), (1536, 128))
VMEM_LIMIT = 66_000_000
ANY = pl.BlockSpec(memory_space=pl.ANY)
WHOLE = pl.BlockSpec(memory_space=pltpu.VMEM)


def dot(a, b):
    return jnp.dot(a, b, preferred_element_type=F32)


def dot_nt(a, b):
    return lax.dot_general(a, b, (((1,), (1,)), ((), ())), preferred_element_type=F32)


def norm(h):
    wide = h.astype(F32)
    scale = lax.rsqrt(jnp.mean(wide * wide, -1, keepdims=True) + 1e-6)
    return wide, scale


def gated(g):
    sig = 0.5 + 0.5 * jnp.tanh(0.5 * g)
    return sig, g * sig


def rows(n):
    return pl.BlockSpec((TILE, n), lambda i: (i, 0))


class Place:
    def __init__(self):
        s, z = lax.axis_index("s"), lax.axis_index("r")
        self.s, self.z = s, z
        self.x, self.y, self.c = s // 4, (s // 2) % 2, s % 2
        x, y, c = self.x, self.y, self.c
        self.partner = x * 4 + y * 2 + (1 - c)
        self.nx = (1 - x) * 4 + y * 2 + c
        self.ny = x * 4 + (1 - y) * 2 + c
        self.diag = (1 - x) * 4 + (1 - y) * 2 + c

    def at(self, s, z=None):
        return (0, self.z if z is None else z, s)


def copy_to(src, dst, send, recv, device):
    return pltpu.make_async_remote_copy(
        src_ref=src, dst_ref=dst, send_sem=send, recv_sem=recv, device_id=device, device_id_type=pl.DeviceIdType.MESH
    )


def signal(barrier, device):
    pl.semaphore_signal(barrier, inc=1, device_id=device, device_id_type=pl.DeviceIdType.MESH)


EARLY = 768
GATHERED = ((0, 0, 0, EARLY), (1, 0, 0, EARLY), (0, 0, EARLY, FF - EARLY), (1, 0, EARLY, FF - EARLY), (2, 0, 0, D))
GATHERED += ((0, 1, 0, FF), (1, 1, 0, FF), (2, 1, 0, D))
NG = len(GATHERED)
FORWARD_STEPS = 3 * TILES
OWN, PASS, DIAG, DONE = range(4)
GATHER_PLAN = {
    0: ((OWN, 0, 1), (PASS, 0, 1), (OWN, 2, 3), (DIAG, 0, 1), (DONE, 0, 1)),
    2: ((PASS, 2, 3), (OWN, 4, 5)),
    4: ((DIAG, 2, 3), (DONE, 2, 3)),
    5: ((PASS, 4), (OWN, 6)),
    6: ((PASS, 5), (OWN, 7)),
    8: ((DIAG, 4), (DONE, 4)),
    9: ((PASS, 6),),
    10: ((DIAG, 5),),
    11: ((PASS, 7),),
    12: ((DIAG, 6, 7), (DONE, 5, 6, 7)),
}


def forward_kernel(og, ou, od, x_ref, h1_ref, act_ref, a_ref, *refs):
    keep, later = refs[:3], refs[3:6]
    w0 = refs[6:9]
    acts, norms = refs[9:11]
    send, recv, local = refs[11:14]
    own = (og, ou, od)
    step = pl.program_id(0)
    p = Place()

    def block(i, slot):
        m, layer, lo, n = GATHERED[i]
        return (later if layer else w0)[m].at[slot, :, pl.ds(lo, n)]

    def cp(i, k):
        m, layer, lo, n = GATHERED[i]
        mine = own[m].at[layer, :, pl.ds(lo, n)]
        src, slot, device = (
            (mine, p.s, p.nx),
            (mine, p.s, p.ny),
            (mine, p.s, p.partner),
            (block(i, p.nx), p.nx, p.partner),
            (block(i, p.ny), p.ny, p.partner),
            (block(i, p.nx), p.nx, p.ny) if i % 2 == 0 else (block(i, p.ny), p.ny, p.nx),
            (block(i, p.diag), p.diag, p.partner),
        )[k]
        return copy_to(src, block(i, slot), send.at[i, k], recv.at[i, k], p.at(device))

    def do(what, i):
        if what == OWN:
            for k in range(3):
                cp(i, k).start()
        elif what == PASS:
            first, then = (0, 1) if i % 2 == 0 else (1, 0)
            cp(i, first).wait_recv()
            cp(i, 5).start()
            cp(i, 3 + first).start()
            cp(i, then).wait_recv()
            cp(i, 3 + then).start()
        elif what == DIAG:
            cp(i, 5).wait_recv()
            cp(i, 6).start()
        else:
            for k in (2, 3, 4, 6):
                cp(i, k).wait_recv()

    def follow(now):
        for what, *items in GATHER_PLAN[now]:
            for i in items:
                do(what, i)

    def own_out(m):
        return pltpu.make_async_copy(own[m].at[1], later[m].at[p.s], local.at[m])

    def w0_out(m):
        return pltpu.make_async_copy(w0[m], keep[m], local.at[3 + m])

    def act_out(t):
        return pltpu.make_async_copy(acts.at[t], act_ref.at[pl.ds(t * TILE, TILE)], local.at[6 + t])

    def norm_out(t):
        return pltpu.make_async_copy(norms.at[t], a_ref.at[pl.ds(t * TILE, TILE)], local.at[6 + TILES + t])

    @pl.when(step == 0)
    def _():
        barrier = pltpu.get_barrier_semaphore()
        for n in (p.partner, p.nx, p.ny):
            signal(barrier, p.at(n))
        pl.semaphore_wait(barrier, 3)
        for m in range(3):
            w0[m][p.s] = own[m][0]
            own_out(m).start()

    @pl.when(step < TILES)
    def _():
        wide, scale = norm(x_ref[...])
        norms[step] = (wide * scale).astype(BF16)

    for now in GATHER_PLAN:
        if now < FORWARD_STEPS:
            pl.when(step == now)(functools.partial(follow, now))

    def up(t, lo, n):
        g = dot(norms[t], w0[0][:, :, lo : lo + n].reshape(D, n))
        u = dot(norms[t], w0[1][:, :, lo : lo + n].reshape(D, n))
        acts[t, :, lo : lo + n] = (gated(g)[1] * u).astype(BF16)

    @pl.when(step < TILES)
    def _():
        up(step, 0, EARLY)

    @pl.when((step >= TILES) & (step < 2 * TILES))
    def _():
        up(step - TILES, EARLY, FF - EARLY)

    @pl.when(step >= 2 * TILES)
    def _():
        mm = dot(acts[step - 2 * TILES], w0[2][...].reshape(FF, D)).astype(BF16).astype(F32)
        h1_ref[...] = (x_ref[...].astype(F32) + mm).astype(BF16)

    for k in range(TILES):

        @pl.when(step == TILES + 1 + k)
        def _(k=k):
            act_out(k).start()
            norm_out(k).start()

    @pl.when(step == 2 * TILES + 1)
    def _():
        for m in range(3):
            w0_out(m).start()

    @pl.when(step == FORWARD_STEPS - 1)
    def _():
        follow(FORWARD_STEPS)
        for i in range(NG):
            for k in range(7):
                cp(i, k).wait_send()
        for m in range(3):
            own_out(m).wait()
            w0_out(m).wait()
        for k in range(TILES):
            act_out(k).wait()
            norm_out(k).wait()


def forward(x, weights):
    blocks = [jax.ShapeDtypeStruct((8,) + w.shape[1:], BF16) for w in weights]
    h1, act, a, *full = pl.pallas_call(
        forward_kernel,
        grid=(FORWARD_STEPS,),
        out_shape=[
            jax.ShapeDtypeStruct((TOK, D), BF16),
            jax.ShapeDtypeStruct((TOK, FF), BF16),
            jax.ShapeDtypeStruct((TOK, D), BF16),
        ]
        + blocks * 2,
        in_specs=[WHOLE, WHOLE, WHOLE, pl.BlockSpec((TILE, D), lambda n: (jnp.where(n < TILES, n, jnp.maximum(n - 2 * TILES, 0)), 0))],
        out_specs=[pl.BlockSpec((TILE, D), lambda n: (jnp.maximum(n - 2 * TILES, 0), 0))] + [ANY] * 8,
        scratch_shapes=[pltpu.VMEM(b.shape, BF16) for b in blocks]
        + [pltpu.VMEM((TILES, TILE, FF), BF16), pltpu.VMEM((TILES, TILE, D), BF16)]
        + [pltpu.SemaphoreType.DMA((NG, 7)), pltpu.SemaphoreType.DMA((NG, 7)), pltpu.SemaphoreType.DMA((6 + 2 * TILES,))],
        compiler_params=pltpu.CompilerParams(
            collective_id=0, has_side_effects=True, vmem_limit_bytes=VMEM_LIMIT, dimension_semantics=("arbitrary",)
        ),
        name="forward",
    )(*weights, x)
    full = [o.reshape(8 * o.shape[1], o.shape[2]) for o in full]
    return h1, act, a, full[:3], full[3:]


def layer1_kernel(h_ref, dy_ref, act0_ref, wg, wu, wd, dh_ref, og, ou, od, od0, accg, accu, accd, accd0, dgs, dus):
    i = pl.program_id(0)

    @pl.when(i == 0)
    def _():
        for acc in (accg, accu, accd, accd0):
            acc[...] = jnp.zeros_like(acc)

    wide, scale = norm(h_ref[...])
    a = (wide * scale).astype(BF16)
    a_t = a.T
    dy = dy_ref[...]
    dy_t = dy.T
    for lo, n in CHUNKS:
        cut = slice(lo, lo + n)
        g = dot(a, wg[:, cut])
        u = dot(a, wu[:, cut])
        da = dot_nt(dy, wd[cut, :]).astype(BF16).astype(F32)
        sig, si = gated(g)
        act = (si * u).astype(BF16)
        du = (da * si).astype(BF16)
        dg = (da * u * (sig + si * (1.0 - sig))).astype(BF16)
        dgs[:, cut] = dg
        dus[:, cut] = du
        accd[:, cut] += dot(dy_t, act)
        accg[:, cut] += dot(a_t, dg)
        accu[:, cut] += dot(a_t, du)
    dn = (dot_nt(dgs[...], wg[...]) + dot_nt(dus[...], wu[...])).astype(BF16).astype(F32)
    inner = jnp.sum(dn * wide, -1, keepdims=True) * (scale * scale * scale * (1.0 / D))
    by_norm = (dn * scale - wide * inner).astype(BF16).astype(F32)
    dh = (dy.astype(F32) + by_norm).astype(BF16)
    dh_ref[...] = dh
    accd0[...] += dot(dh.T, act0_ref[...])

    @pl.when(i == TILES - 1)
    def _():
        og[...] = accg[...].astype(BF16)
        ou[...] = accu[...].astype(BF16)
        for acc, out in ((accd, od), (accd0, od0)):
            for h in range(4):
                t = acc[128 * h : 128 * h + 128, :].T.astype(BF16)
                for s in range(8):
                    out[s, h] = t[208 * s : 208 * s + 208]


def layer1(h1, dy, act0, w):
    up, down = jax.ShapeDtypeStruct((D, FF), BF16), jax.ShapeDtypeStruct((8, 4, 208, 128), BF16)
    return pl.pallas_call(
        layer1_kernel,
        grid=(TILES,),
        out_shape=[jax.ShapeDtypeStruct((TOK, D), BF16), up, up, down, down],
        in_specs=[rows(D), rows(D), rows(FF), WHOLE, WHOLE, WHOLE],
        out_specs=[rows(D), WHOLE, WHOLE, WHOLE, WHOLE],
        scratch_shapes=[pltpu.VMEM((D, FF), F32)] * 4 + [pltpu.VMEM((TILE, FF), BF16)] * 2,
        compiler_params=pltpu.CompilerParams(vmem_limit_bytes=VMEM_LIMIT, dimension_semantics=("arbitrary",)),
        name="layer1",
    )(h1, dy, act0, *w)


BULK = ((16, FF),) * 4 + ((208, 128),) * 4
PIECES = BULK + tuple((32, n) for _, n in CHUNKS for _ in range(2))
NP = len(PIECES)
NBUF = 10
DIRECT = NP - 2


def schedule():
    plan = []

    def put(pieces, *steps):
        for piece in pieces:
            for stage, step in enumerate(steps + (99,) * (LAST + 1 - len(steps))):
                plan.append((min(step, STEPS), stage, piece))

    put((0, 1), 0, 0, 2, 4, 6, 8)
    put((2, 3), 0, 1, 3, 6, 8, 10)
    put((4, 5), 0, 2, 5, 8, 10, 12)
    put((6, 7), 0, 3, 7, 9, 11, 13)
    put((8, 9), 4, 5, 8, 10, 12, 14)
    put((10, 11), 8, 9, 11, 13, 15)
    put((12, 13), 12, 13, 15)
    put((14, 15), 16)
    def rank(e):
        step, stage, piece = e
        if step == STEPS:
            return (step, (0, 1, 3.5, 5.5, 9, 9, 9)[stage] if piece >= DIRECT else max(stage, 2.5), piece)
        return (step, stage, piece) if step == 0 else (step, piece // 2, stage, piece)

    return sorted(plan, key=rank)


LAST = 6
STEPS = len(CHUNKS) * TILES


def backward0_kernel(*refs):
    a_ref, dh_ref = refs[:2]
    hbm_w = refs[2:5]
    bulk = refs[5:9]
    og, ou, od = refs[9:12]
    a_t, accg, accu = refs[12:15]
    chunk_g = refs[15 : 15 + 2 * len(CHUNKS)]
    at = 15 + 2 * len(CHUNKS)
    bulk_own = refs[at : at + 8]
    at += 8
    bufs = [refs[at + NBUF * k : at + NBUF * (k + 1)] for k in range(NP)]
    wg, wu, wd, send, recv, local = refs[at + NBUF * NP :]
    loads = lambda: [pltpu.make_async_copy(a, b, local.at[8 + n]) for n, (a, b) in enumerate(zip(hbm_w, (wg, wu, wd), strict=True))]

    j, i = pl.program_id(0), pl.program_id(1)
    step = j * TILES + i
    p = Place()
    z = p.z
    beside, across = z + 1 - 2 * (z % 2), 3 - z
    half_beside, half_across = (z + z // 2) % 2, z // 2

    @pl.when(step == 0)
    def _():
        barrier = pltpu.get_barrier_semaphore()
        for n in (p.partner, p.nx, p.ny, p.diag):
            signal(barrier, p.at(n))
        for n in range(1, 4):
            signal(barrier, p.at(p.s, lax.rem(z + n, 4)))
        pl.semaphore_wait(barrier, 7)
        for cp in loads():
            cp.start()

    def piece_stage(k, stage):
        r0, s1, r1, s2, r2, zs, zr, zt, zp, fin = bufs[k]
        one, two_, half = (beside, across, half_beside) if (k // 2) % 2 == 0 else (across, beside, half_across)
        other = 1 - half
        x_first = k % 2 == 0
        mine, theirs = (p.x, 1 - p.x) if x_first else (p.y, 1 - p.y)
        mine_b, theirs_b = (p.y, 1 - p.y) if x_first else (p.x, 1 - p.x)
        na, nb = (p.nx, p.ny) if x_first else (p.ny, p.nx)

        def chip(first, second):
            return (first, second) if x_first else (second, first)

        if k < 8:
            source = bulk[k // 2].at[:, :, 1 - p.c, k % 2]
            own_half = lambda: pltpu.make_async_copy(bulk[k // 2].at[:, :, p.c, k % 2], bulk_own[k], local.at[k])
            term = lambda u, v: bulk_own[k][u, v].astype(F32)
            term_half = lambda u, v, h: bulk_own[k][u, v, h].astype(F32)
        else:
            source = chunk_g[k - 8].at[:, :, 1 - p.c]
            own_half = None
            term = lambda u, v: chunk_g[k - 8][u, v, p.c].astype(F32)
            term_half = lambda u, v, h: chunk_g[k - 8][u, v, p.c, h].astype(F32)

        def two(first, second):
            u, v = chip(first, second)
            return term(u, v) + r0[u, v].astype(F32)

        cps = (
            lambda: copy_to(source, r0, send.at[k, 0], recv.at[k, 0], p.at(p.partner)),
            lambda: copy_to(s1, r1, send.at[k, 1], recv.at[k, 1], p.at(na)),
            lambda: copy_to(s2, r2, send.at[k, 2], recv.at[k, 2], p.at(nb)),
        )
        def finish():
            for h in range(2):
                if k < 4:
                    lo = 32 * (k % 2) + 16 * h
                    (og, ou)[k // 2][1, lo : lo + 16, :] = fin[h]
                elif k < 8:
                    lo = 256 * (k % 2) + 128 * h
                    od[(7 - k) // 2, :, lo : lo + 128] = fin[h]
                else:
                    lo, n = CHUNKS[(k - 8) // 2]
                    (og, ou)[k % 2][0, 32 * h : 32 * h + 32, lo : lo + n] = fin[h]

        if k >= DIRECT:
            chips = ((1 - p.x, p.y), (p.x, 1 - p.y), (1 - p.x, 1 - p.y))
            across_chips = [
                lambda n=n, u=u, v=v: copy_to(
                    s1.at[n], r1.at[n], send.at[k, 1 + n], recv.at[k, 1 + n], p.at(u * 4 + v * 2 + p.c)
                )
                for n, (u, v) in enumerate(chips)
            ]
            along = [
                lambda n=n: copy_to(zs.at[z], zs.at[z], send.at[k, 4 + n], recv.at[k, 4 + n], p.at(p.s, lax.rem(z + 1 + n, 4)))
                for n in range(3)
            ]
            arrived = [
                lambda n=n: copy_to(zs.at[lax.rem(z + 3 - n, 4)], zs.at[lax.rem(z + 3 - n, 4)], send.at[k, 4 + n], recv.at[k, 4 + n], p.at(p.s, lax.rem(z + 3 - n, 4)))
                for n in range(3)
            ]
            if stage == 0:
                cps[0]().start()
            if stage == 1:
                cps[0]().wait_recv()
                for n in (2, 0, 1):
                    s1[n] = two(*chip(*chips[n])).astype(BF16)
                    across_chips[n]().start()
            if stage == 2:
                for cp in across_chips:
                    cp().wait_recv()
                total = two(*chip(p.x, p.y))
                for n in range(3):
                    total += r1[n].astype(F32)
                zs[z] = total.astype(BF16)
                for cp in along:
                    cp().start()
            if stage == 3:
                for cp in arrived:
                    cp().wait_recv()
                total = zs[0].astype(F32) + zs[1].astype(F32) + zs[2].astype(F32) + zs[3].astype(F32)
                fin[...] = total.astype(BF16)
                finish()
            if stage == 4:
                for cp in [cps[0]] + across_chips + along:
                    cp().wait_send()
            return

        if stage == 0:
            cps[0]().start()
            if own_half is not None:
                own_half().start()
        if stage == 1:
            cps[0]().wait_recv()
            if own_half is not None:
                own_half().wait()
            for q in range(2):
                s1[q] = two(theirs, q).astype(BF16)
            cps[1]().start()
        if stage == 2:
            cps[1]().wait_recv()
            s2[...] = (two(mine, theirs_b) + r1[theirs_b].astype(F32)).astype(BF16)
            cps[2]().start()
        z_cps = (
            lambda: copy_to(zs, zr, send.at[k, 3], recv.at[k, 3], p.at(p.s, one)),
            lambda: copy_to(zt, zp, send.at[k, 4], recv.at[k, 4], p.at(p.s, two_)),
            lambda: copy_to(fin.at[half], fin.at[half], send.at[k, 5], recv.at[k, 5], p.at(p.s, one)),
        )

        def xy_sum(h):
            u, v = chip(mine, mine_b)
            return term_half(u, v, h) + r0[u, v, h].astype(F32) + r1[mine_b, h].astype(F32) + r2[h].astype(F32)

        if stage == 3:
            cps[2]().wait_recv()
            zs[...] = xy_sum(other).astype(BF16)
            z_cps[0]().start()
        if stage == 4:
            z_cps[0]().wait_recv()
            zt[...] = (xy_sum(half) + zr[...].astype(F32)).astype(BF16)
            z_cps[1]().start()
        if stage == 5:
            z_cps[1]().wait_recv()
            fin[half] = (zt[...].astype(F32) + zp[...].astype(F32)).astype(BF16)
            z_cps[2]().start()
        if stage == 6:
            copy_to(fin.at[other], fin.at[other], send.at[k, 5], recv.at[k, 5], p.at(p.s, one)).wait_recv()
            for cp in z_cps:
                cp().wait_send()
            for cp in cps:
                cp().wait_send()
            finish()

    plan = schedule()

    def events(now):
        for when, stage, k in plan:
            if when == now:
                piece_stage(k, stage)

    for now in sorted({e[0] for e in plan if e[0] < STEPS}):
        pl.when(step == now)(functools.partial(events, now))

    @pl.when(step == 0)
    def _():
        for cp in loads():
            cp.wait()

    @pl.when(j == 0)
    def _():
        a_t[i] = a_ref[...].T

    def body(n, lo, first):
        a, dh = a_ref[...], dh_ref[...]
        cut = pl.ds(lo, n)
        g = dot(a, wg[:, cut])
        u = dot(a, wu[:, cut])
        da = dot_nt(dh, wd[cut, :]).astype(BF16).astype(F32)
        sig, si = gated(g)
        du = (da * si).astype(BF16)
        dg = (da * u * (sig + si * (1.0 - sig))).astype(BF16)
        at_tile = a_t[i]
        pg, pu = dot(at_tile, dg), dot(at_tile, du)

        @pl.when(i == 0)
        def _():
            accg[:, :n] = pg
            accu[:, :n] = pu

        @pl.when(i > 0)
        def _():
            accg[:, :n] += pg
            accu[:, :n] += pu

    @pl.when(j < 3)
    def _():
        body(512, pl.multiple_of(j * 512, 512), None)

    @pl.when(j == 3)
    def _():
        body(128, 1536, None)

    for k, (lo, n) in enumerate(CHUNKS):

        @pl.when((j == k) & (i == TILES - 1))
        def _(k=k, n=n):
            for acc, out in ((accg, chunk_g[2 * k]), (accu, chunk_g[2 * k + 1])):
                for q in range(16):
                    c_, h_ = (q // 2) % 2, q % 2
                    out[q // 8, (q // 4) % 2, c_, h_] = acc[32 * q : 32 * q + 32, :n].astype(BF16)

    pl.when(step == STEPS - 1)(functools.partial(events, STEPS))


def backward0(a0, dh1, w, bulk):
    tile2 = lambda n: pl.BlockSpec((TILE, n), lambda j, i: (i, 0))
    bufs = []
    for k, (hr, hc) in enumerate(PIECES):
        one, four = (hr, hc), (2, 2, hr, hc)
        if k < DIRECT:
            shapes = (2,) + four, four, four, (2,) + one, (2,) + one, one, one, one, one, (2,) + one
        else:
            shapes = (2,) + four, (3, 2) + one, (3, 2) + one, one, one, (4, 2) + one, one, one, one, (2,) + one
        bufs += [pltpu.VMEM(shape, BF16) for shape in shapes]
    up, down = jax.ShapeDtypeStruct((2, 64, FF), BF16), jax.ShapeDtypeStruct((2, 208, D), BF16)
    bulk = [t.reshape((2, 2, 2, 2, 2) + shape) for t, shape in zip(bulk, BULK[::2], strict=True)]
    return pl.pallas_call(
        backward0_kernel,
        grid=(len(CHUNKS), TILES),
        out_shape=[up, up, down],
        in_specs=[tile2(D), tile2(D)] + [ANY] * 7,
        out_specs=[WHOLE] * 3,
        scratch_shapes=[pltpu.VMEM((TILES, D, TILE), BF16)]
        + [pltpu.VMEM((D, 512), F32)] * 2
        + [pltpu.VMEM((2, 2, 2, 2, 32, n), BF16) for _, n in CHUNKS for _ in range(2)]
        + [pltpu.VMEM((2, 2, 2) + shape, BF16) for shape in BULK]
        + bufs
        + [pltpu.VMEM((D, FF), BF16), pltpu.VMEM((D, FF), BF16), pltpu.VMEM((FF, D), BF16)]
        + [pltpu.SemaphoreType.DMA((NP, 7)), pltpu.SemaphoreType.DMA((NP, 7)), pltpu.SemaphoreType.DMA((11,))],
        compiler_params=pltpu.CompilerParams(
            collective_id=1, has_side_effects=True, vmem_limit_bytes=VMEM_LIMIT, dimension_semantics=("arbitrary", "arbitrary")
        ),
        name="backward0",
    )(a0, dh1, *w, *bulk)


def adamw(w, m, v, g):
    m = 0.9 * m + 0.1 * g
    v = 0.95 * v + 0.05 * g * g
    step = m * lax.rsqrt(v + 1e-8) + 0.1 * w
    return (w - 0.02 * step).astype(BF16), m, v


def solution(mesh):
    def step(x, dy, *arrays):
        weights, m, v = (arrays[i : i + 3] for i in (0, 3, 6))
        h1, act0, a0, w0, w1 = forward(x[0], weights)
        dh1, *bulk = layer1(h1, dy[0], act0, w1)
        gradients = backward0(a0, dh1, w0, bulk)
        new = [adamw(w.astype(F32), m, v, g.astype(F32)) for w, m, v, g in zip(weights, m, v, gradients, strict=True)]
        return tuple(one[which] for which in range(3) for one in new)

    states, cut = P(("rep", "r", "s"), None, None), P(None, "s", None)
    return jax.shard_map(
        step,
        mesh=mesh,
        in_specs=(states, states) + (cut,) * 9,
        out_specs=(P("rep", "s", None),) * 9,
        check_vma=False,
    )
```

time: 280 us -> 248 us (0.89)
  Pallas kernels: 268 us -> 240 us
  local copies, waits for them, and re-layouts: 4.85 us -> 0.05 us
    pallas_call x2 -> x1, Pallas kernels: 76.9 us -> 60 us  [forward(): pl.pallas_call(forward_kernel, grid=(FORWARD_STEPS,), out_shape=[jax.Shap...]
    pallas_call x1, Pallas kernels: 101 us -> 91.6 us  [backward0(): pl.pallas_call(backward0_kernel, grid=(len(CHUNKS), TILES), out_shape=[up...]
    squeeze x2 -> x0, local copies, waits for them, and re-layouts: 3.98 us -> none  [gather(): own = [w[l] for l in range(2) for w in weights]]
    convert_element_type x3 -> x2, other arithmetic: 6.38 us -> 6.75 us  [adamw(): return ((w - 0.02 * step).astype(BF16), m, v)]
where the time goes in v2:
time: 248 us; the launch traced here: 247 us
  Pallas kernels  240 us (97%)
  other arithmetic  6.75 us (3%)
    pallas_call x1, Pallas kernels, backward0(): pl.pallas_call(backward0_kernel, grid=(len(CHUNKS), TILES), out_shape=[up...  91.6 us
    pallas_call x1, Pallas kernels, layer1(): pl.pallas_call(layer1_kernel, grid=(TILES,), out_shape=[jax.ShapeDtypeStr...  88.3 us
    pallas_call x1, Pallas kernels, forward(): pl.pallas_call(forward_kernel, grid=(FORWARD_STEPS,), out_shape=[jax.Shap...  60 us
    convert_element_type x2, other arithmetic, adamw(): return ((w - 0.02 * step).astype(BF16), m, v)  6.75 us

profile of v2, /device:TPU:0, one launch (start us, length us, event | category | flops | bytes accessed | tf_op | source)
XLA Modules:
  0.0 247.5 jit_solution(7258098413984193909)
XLA Ops:
  0.6 60.0 %forward.1 = (bf16[4096,512]{1,0:T(8,128)(2,1)}, bf16[4096,1664]{1,0:T(8,128)(2,1)}, bf16[4096,512]{1,0:T(8,128)(2,1)}, bf16[8,64,1664]{2,1,0:T(8,128)(2,1)}, bf...) custom-call(bf16[2,64,1664]{2,1,0:T(8,128)(2,1)} %og.1, ...), custom_call_target="tpu_custom_call" | custom-call | tf_op jit(solution)/shard_map/forward/pallas_call | solution.py:215
  60.7 88.3 %layer1.1 = (bf16[4096,512]{1,0:T(8,128)(2,1)}, bf16[512,1664]{1,0:T(8,128)(2,1)}, bf16[512,1664]{1,0:T(8,128)(2,1)}, bf16[8,4,208,128]{3,2,1,0:T(8,128)(2,1)}, bf16[8,4,208,128]{3,2,1,0:T(8,128)(2,1)}) custom-call(bf16[4096,512]{1,0:T(8,128)(2,1)} %get-tuple-element.27.h_ref, bf16[4096,512]{1,0:T(8,128)(2,1)} %bitcast.12, ...), custom_call_target="tpu_custom_call" | custom-call | tf_op jit(solution)/shard_map/layer1/pallas_call | solution.py:285
  149.0 0.0 copy-start
  149.0 91.6 %backward0.1 = (bf16[2,64,1664]{2,1,0:T(8,128)(2,1)}, bf16[2,64,1664]{2,1,0:T(8,128)(2,1)}, bf16[2,208,512]{2,1,0:T(8,128)(2,1)}) custom-call(bf16[4096,512]{1,0:T(8,128)(2,1)} %get-tuple-element.26.refs_0_, bf16[4096,512]{1,0:T(8,128)(2,1)} %get-tuple-element.32.refs_1_, bf16[512,1664]{1,0:T(8,128)(2,1)} %bitcast.14, bf16[512,1664]{1,0:T(8,128)(2,1)} %bitcast.15, ...), custom_call_target="tpu_custom_call" | custom-call | tf_op jit(solution)/shard_map/backward0/pallas_call | solution.py:570
  240.6 0.0 copy-done
  240.6 0.0 copy-start.1
  240.6 0.0 copy-start.2
  240.6 0.0 copy-start.3
  240.6 0.0 copy-start.4
  240.6 0.0 copy-start.5
  240.7 0.0 copy-start.6
  240.7 0.0 copy-start.7
  240.7 3.3 %fusion.10 = (bf16[2,208,512]{2,1,0:T(8,128)(2,1)}, f32[2,208,512]{2,1,0:T(8,128)}, f32[2,208,512]{2,1,0:T(8,128)}) fusion(bf16[2,208,512]{2,1,0:T(8,128)(2,1)S(1)} %copy-done, bf16[2,208,512]{2,1,0:T(8,128)(2,1)} %get-tuple-element.42, f32[2,208,512]{2,1,0:T(8,128)} %param.21, f32[2,208,512]{2,1,0:T(8,128)} %param.18), kind=kLoop, calls=%fused_computation.22 | loop fusion | flops 3407872 | bytes 4685824 | tf_op jit(solution)/shard_map/convert_element_type | solution.py:594
  244.0 0.0 copy-done.1
  244.0 0.0 copy-done.2
  244.0 0.0 copy-done.3
  244.0 0.0 copy-done.4
  244.0 0.0 copy-done.5
  244.0 0.0 copy-done.6
  244.0 0.0 copy-done.7
  244.0 3.5 %fusion.2 = (bf16[2,64,1664]{2,1,0:T(8,128)(2,1)}, f32[2,64,1664]{2,1,0:T(8,128)}, f32[2,64,1664]{2,1,0:T(8,128)}, bf16[2,64,1664]{2,1,0:T(8,128)(2,1)}, f32[2,64,1664]{2,1,0:T(8,128)}, /*index=5*/f32[2,64,1664]{2,1,0:T(8,128)}) fusion(bf16[2,64,1664]{2,1,0:T(8,128)(2,1)S(1)} %copy-done.1, bf16[2,64,1664]{2,1,0:T(8,128)(2,1)S(1)} %copy-done.7, ...), kind=kLoop, calls=%fused_computation.14 | loop fusion | flops 6815744 | bytes 9371648 | tf_op jit(solution)/shard_map/convert_element_type | solution.py:594
Async XLA Ops:
  149.0 91.6 %copy-start = (bf16[2,208,512]{2,1,0:T(8,128)(2,1)S(1)}, bf16[2,208,512]{2,1,0:T(8,128)(2,1)}, u32[]{:S(2)}) copy-start(bf16[2,208,512]{2,1,0:T(8,128)(2,1)} %od.1) | copy-start | bytes 1277956
  240.6 3.4 %copy-start.1 = (bf16[2,64,1664]{2,1,0:T(8,128)(2,1)S(1)}, bf16[2,64,1664]{2,1,0:T(8,128)(2,1)}, u32[]{:S(2)}) copy-start(bf16[2,64,1664]{2,1,0:T(8,128)(2,1)} %og.1) | copy-start | bytes 1277956
  240.6 3.3 %copy-start.2 = (bf16[2,64,1664]{2,1,0:T(8,128)(2,1)S(1)}, bf16[2,64,1664]{2,1,0:T(8,128)(2,1)}, u32[]{:S(2)}) copy-start(bf16[2,64,1664]{2,1,0:T(8,128)(2,1)} %ou.1) | copy-start | bytes 1277956
  240.6 3.3 %copy-start.3 = (f32[2,64,1664]{2,1,0:T(8,128)S(1)}, f32[2,64,1664]{2,1,0:T(8,128)}, u32[]{:S(2)}) copy-start(f32[2,64,1664]{2,1,0:T(8,128)} %param.19) | copy-start | bytes 2555908
  240.6 3.3 %copy-start.4 = (f32[2,64,1664]{2,1,0:T(8,128)S(1)}, f32[2,64,1664]{2,1,0:T(8,128)}, u32[]{:S(2)}) copy-start(f32[2,64,1664]{2,1,0:T(8,128)} %param.16) | copy-start | bytes 2555908
  240.6 3.3 %copy-start.5 = (f32[2,64,1664]{2,1,0:T(8,128)S(1)}, f32[2,64,1664]{2,1,0:T(8,128)}, u32[]{:S(2)}) copy-start(f32[2,64,1664]{2,1,0:T(8,128)} %param.20) | copy-start | bytes 2555908
  240.7 3.3 %copy-start.6 = (f32[2,64,1664]{2,1,0:T(8,128)S(1)}, f32[2,64,1664]{2,1,0:T(8,128)}, u32[]{:S(2)}) copy-start(f32[2,64,1664]{2,1,0:T(8,128)} %param.17) | copy-start | bytes 2555908
  240.7 3.3 %copy-start.7 = (bf16[2,64,1664]{2,1,0:T(8,128)(2,1)S(1)}, bf16[2,64,1664]{2,1,0:T(8,128)(2,1)}, u32[]{:S(2)}) copy-start(bf16[2,64,1664]{2,1,0:T(8,128)(2,1)} %get-tuple-element.40) | copy-start | bytes 1277956

commit v3 on v2

--- a/solution.py
+++ b/solution.py
@@ -10,11 +10,16 @@
 F32, BF16 = jnp.float32, jnp.bfloat16
 D, FF, TOK = 512, 1664, 4096
 TILE = 1024
+STRIP = 256
 TILES = TOK // TILE
 CHUNKS = ((0, 512), (512, 512), (1024, 512), (1536, 128))
 VMEM_LIMIT = 66_000_000
 ANY = pl.BlockSpec(memory_space=pl.ANY)
 WHOLE = pl.BlockSpec(memory_space=pltpu.VMEM)
+
+
+def pieces_of(lo, n):
+    return [(lo + at, min(STRIP, n - at)) for at in range(0, n, STRIP)]
 
 
 def dot(a, b):
@@ -46,10 +51,15 @@
         self.s, self.z = s, z
         self.x, self.y, self.c = s // 4, (s // 2) % 2, s % 2
         x, y, c = self.x, self.y, self.c
-        self.partner = x * 4 + y * 2 + (1 - c)
-        self.nx = (1 - x) * 4 + y * 2 + c
-        self.ny = x * 4 + (1 - y) * 2 + c
-        self.diag = (1 - x) * 4 + (1 - y) * 2 + c
+        self.x_, self.y_, self.c_ = 1 - x, 1 - y, 1 - c
+        self.partner = self.core(x, y, self.c_)
+        self.nx = self.core(self.x_, y, c)
+        self.ny = self.core(x, self.y_, c)
+        self.diag = self.core(self.x_, self.y_, c)
+
+    @staticmethod
+    def core(x, y, c):
+        return x * 4 + y * 2 + c
 
     def at(self, s, z=None):
         return (0, self.z if z is None else z, s)
@@ -66,8 +76,8 @@
 
 
 EARLY = 768
-GATHERED = ((0, 0, 0, EARLY), (1, 0, 0, EARLY), (0, 0, EARLY, FF - EARLY), (1, 0, EARLY, FF - EARLY), (2, 0, 0, D))
-GATHERED += ((0, 1, 0, FF), (1, 1, 0, FF), (2, 1, 0, D))
+GATHERED = tuple((m, 0, lo, n) for lo, n in ((0, EARLY), (EARLY, FF - EARLY)) for m in (0, 1)) + ((2, 0, 0, D),)
+GATHERED += tuple((m, 1, 0, n) for m, n in enumerate((FF, FF, D)))
 NG = len(GATHERED)
 FORWARD_STEPS = 3 * TILES
 OWN, PASS, DIAG, DONE = range(4)
@@ -167,9 +177,11 @@
             pl.when(step == now)(functools.partial(follow, now))
 
     def up(t, lo, n):
-        g = dot(norms[t], w0[0][:, :, lo : lo + n].reshape(D, n))
-        u = dot(norms[t], w0[1][:, :, lo : lo + n].reshape(D, n))
-        acts[t, :, lo : lo + n] = (gated(g)[1] * u).astype(BF16)
+        for at, width in pieces_of(lo, n):
+            cut = slice(at, at + width)
+            g = dot(norms[t], w0[0][:, :, cut].reshape(D, width))
+            u = dot(norms[t], w0[1][:, :, cut].reshape(D, width))
+            acts[t, :, cut] = (gated(g)[1] * u).astype(BF16)
 
     @pl.when(step < TILES)
     def _():
@@ -235,7 +247,7 @@
     return h1, act, a, full[:3], full[3:]
 
 
-def layer1_kernel(h_ref, dy_ref, act0_ref, wg, wu, wd, dh_ref, og, ou, od, od0, accg, accu, accd, accd0, dgs, dus):
+def layer1_kernel(h_ref, dy_ref, act0_ref, wg, wu, wd, dh_ref, og, ou, od, od0, accg, accu, accd, accd0, dgs, dus, acts):
     i = pl.program_id(0)
 
     @pl.when(i == 0)
@@ -248,7 +260,7 @@
     a_t = a.T
     dy = dy_ref[...]
     dy_t = dy.T
-    for lo, n in CHUNKS:
+    for lo, n in pieces_of(0, FF):
         cut = slice(lo, lo + n)
         g = dot(a, wg[:, cut])
         u = dot(a, wu[:, cut])
@@ -259,9 +271,10 @@
         dg = (da * u * (sig + si * (1.0 - sig))).astype(BF16)
         dgs[:, cut] = dg
         dus[:, cut] = du
-        accd[:, cut] += dot(dy_t, act)
-        accg[:, cut] += dot(a_t, dg)
-        accu[:, cut] += dot(a_t, du)
+        acts[:, cut] = act
+    accd[...] += dot(dy_t, acts[...])
+    accg[...] += dot(a_t, dgs[...])
+    accu[...] += dot(a_t, dus[...])
     dn = (dot_nt(dgs[...], wg[...]) + dot_nt(dus[...], wu[...])).astype(BF16).astype(F32)
     inner = jnp.sum(dn * wide, -1, keepdims=True) * (scale * scale * scale * (1.0 / D))
     by_norm = (dn * scale - wide * inner).astype(BF16).astype(F32)
@@ -288,7 +301,7 @@
         out_shape=[jax.ShapeDtypeStruct((TOK, D), BF16), up, up, down, down],
         in_specs=[rows(D), rows(D), rows(FF), WHOLE, WHOLE, WHOLE],
         out_specs=[rows(D), WHOLE, WHOLE, WHOLE, WHOLE],
-        scratch_shapes=[pltpu.VMEM((D, FF), F32)] * 4 + [pltpu.VMEM((TILE, FF), BF16)] * 2,
+        scratch_shapes=[pltpu.VMEM((D, FF), F32)] * 4 + [pltpu.VMEM((TILE, FF), BF16)] * 3,
         compiler_params=pltpu.CompilerParams(vmem_limit_bytes=VMEM_LIMIT, dimension_semantics=("arbitrary",)),
         name="layer1",
     )(h1, dy, act0, *w)
@@ -304,29 +317,29 @@
 def schedule():
     plan = []
 
-    def put(pieces, *steps):
-        for piece in pieces:
-            for stage, step in enumerate(steps + (99,) * (LAST + 1 - len(steps))):
-                plan.append((min(step, STEPS), stage, piece))
-
-    put((0, 1), 0, 0, 2, 4, 6, 8)
-    put((2, 3), 0, 1, 3, 6, 8, 10)
-    put((4, 5), 0, 2, 5, 8, 10, 12)
-    put((6, 7), 0, 3, 7, 9, 11, 13)
-    put((8, 9), 4, 5, 8, 10, 12, 14)
-    put((10, 11), 8, 9, 11, 13, 15)
-    put((12, 13), 12, 13, 15)
-    put((14, 15), 16)
+    def put(pair, *steps):
+        for piece in (pair, pair + 1):
+            for stage in range(STAGES):
+                plan.append((steps[stage] if stage < len(steps) else STEPS, stage, piece))
+
+    put(0, 0, 0, 2, 4, 6, 8)
+    put(2, 0, 1, 3, 6, 8, 10)
+    put(4, 0, 2, 5, 8, 11, 13)
+    put(6, 0, 3, 7, 9, 12, 14)
+    put(8, 4, 5, 8, 10, 13, 15)
+    put(10, 8, 9, 11, 13, 15)
+    put(12, 12, 13, 15)
+    put(14)
     def rank(e):
         step, stage, piece = e
         if step == STEPS:
-            return (step, (0, 1, 3.5, 5.5, 9, 9, 9)[stage] if piece >= DIRECT else max(stage, 2.5), piece)
+            return (step, (stage if stage < 2 else 4 * stage - 1) if piece >= DIRECT else 2 * stage, piece)
         return (step, stage, piece) if step == 0 else (step, piece // 2, stage, piece)
 
     return sorted(plan, key=rank)
 
 
-LAST = 6
+STAGES = 7
 STEPS = len(CHUNKS) * TILES
 
 
@@ -341,7 +354,7 @@
     bulk_own = refs[at : at + 8]
     at += 8
     bufs = [refs[at + NBUF * k : at + NBUF * (k + 1)] for k in range(NP)]
-    wg, wu, wd, send, recv, local = refs[at + NBUF * NP :]
+    wg, wu, wd, dgs, dus, send, recv, local = refs[at + NBUF * NP :]
     loads = lambda: [pltpu.make_async_copy(a, b, local.at[8 + n]) for n, (a, b) in enumerate(zip(hbm_w, (wg, wu, wd), strict=True))]
 
     j, i = pl.program_id(0), pl.program_id(1)
@@ -364,23 +377,26 @@
 
     def piece_stage(k, stage):
         r0, s1, r1, s2, r2, zs, zr, zt, zp, fin = bufs[k]
-        one, two_, half = (beside, across, half_beside) if (k // 2) % 2 == 0 else (across, beside, half_across)
+        one, two_, half = (beside, across, half_beside) if k % 2 == 0 else (across, beside, half_across)
         other = 1 - half
         x_first = k % 2 == 0
-        mine, theirs = (p.x, 1 - p.x) if x_first else (p.y, 1 - p.y)
-        mine_b, theirs_b = (p.y, 1 - p.y) if x_first else (p.x, 1 - p.x)
+        mine, theirs = (p.x, p.x_) if x_first else (p.y, p.y_)
+        mine_b, theirs_b = (p.y, p.y_) if x_first else (p.x, p.x_)
         na, nb = (p.nx, p.ny) if x_first else (p.ny, p.nx)
+
+        def hop(n, src, dst, device):
+            return copy_to(src, dst, send.at[k, n], recv.at[k, n], device)
 
         def chip(first, second):
             return (first, second) if x_first else (second, first)
 
         if k < 8:
-            source = bulk[k // 2].at[:, :, 1 - p.c, k % 2]
+            source = bulk[k // 2].at[:, :, p.c_, k % 2]
             own_half = lambda: pltpu.make_async_copy(bulk[k // 2].at[:, :, p.c, k % 2], bulk_own[k], local.at[k])
             term = lambda u, v: bulk_own[k][u, v].astype(F32)
             term_half = lambda u, v, h: bulk_own[k][u, v, h].astype(F32)
         else:
-            source = chunk_g[k - 8].at[:, :, 1 - p.c]
+            source = chunk_g[k - 8].at[:, :, p.c_]
             own_half = None
             term = lambda u, v: chunk_g[k - 8][u, v, p.c].astype(F32)
             term_half = lambda u, v, h: chunk_g[k - 8][u, v, p.c, h].astype(F32)
@@ -390,9 +406,9 @@
             return term(u, v) + r0[u, v].astype(F32)
 
         cps = (
-            lambda: copy_to(source, r0, send.at[k, 0], recv.at[k, 0], p.at(p.partner)),
-            lambda: copy_to(s1, r1, send.at[k, 1], recv.at[k, 1], p.at(na)),
-            lambda: copy_to(s2, r2, send.at[k, 2], recv.at[k, 2], p.at(nb)),
+            lambda: hop(0, source, r0, p.at(p.partner)),
+            lambda: hop(1, s1, r1, p.at(na)),
+            lambda: hop(2, s2, r2, p.at(nb)),
         )
         def finish():
             for h in range(2):
@@ -407,19 +423,17 @@
                     (og, ou)[k % 2][0, 32 * h : 32 * h + 32, lo : lo + n] = fin[h]
 
         if k >= DIRECT:
-            chips = ((1 - p.x, p.y), (p.x, 1 - p.y), (1 - p.x, 1 - p.y))
+            chips = ((p.x_, p.y), (p.x, p.y_), (p.x_, p.y_))
             across_chips = [
-                lambda n=n, u=u, v=v: copy_to(
-                    s1.at[n], r1.at[n], send.at[k, 1 + n], recv.at[k, 1 + n], p.at(u * 4 + v * 2 + p.c)
-                )
+                lambda n=n, u=u, v=v: hop(1 + n, s1.at[n], r1.at[n], p.at(p.core(u, v, p.c)))
                 for n, (u, v) in enumerate(chips)
             ]
             along = [
-                lambda n=n: copy_to(zs.at[z], zs.at[z], send.at[k, 4 + n], recv.at[k, 4 + n], p.at(p.s, lax.rem(z + 1 + n, 4)))
+                lambda n=n: hop(4 + n, zs.at[z], zs.at[z], p.at(p.s, lax.rem(z + 1 + n, 4)))
                 for n in range(3)
             ]
             arrived = [
-                lambda n=n: copy_to(zs.at[lax.rem(z + 3 - n, 4)], zs.at[lax.rem(z + 3 - n, 4)], send.at[k, 4 + n], recv.at[k, 4 + n], p.at(p.s, lax.rem(z + 3 - n, 4)))
+                lambda n=n, q=lax.rem(z + 3 - n, 4): hop(4 + n, zs.at[q], zs.at[q], p.at(p.s, q))
                 for n in range(3)
             ]
             if stage == 0:
@@ -441,7 +455,7 @@
             if stage == 3:
                 for cp in arrived:
                     cp().wait_recv()
-                total = zs[0].astype(F32) + zs[1].astype(F32) + zs[2].astype(F32) + zs[3].astype(F32)
+                total = jnp.sum(zs[...].astype(F32), 0)
                 fin[...] = total.astype(BF16)
                 finish()
             if stage == 4:
@@ -465,9 +479,9 @@
             s2[...] = (two(mine, theirs_b) + r1[theirs_b].astype(F32)).astype(BF16)
             cps[2]().start()
         z_cps = (
-            lambda: copy_to(zs, zr, send.at[k, 3], recv.at[k, 3], p.at(p.s, one)),
-            lambda: copy_to(zt, zp, send.at[k, 4], recv.at[k, 4], p.at(p.s, two_)),
-            lambda: copy_to(fin.at[half], fin.at[half], send.at[k, 5], recv.at[k, 5], p.at(p.s, one)),
+            lambda: hop(3, zs, zr, p.at(p.s, one)),
+            lambda: hop(4, zt, zp, p.at(p.s, two_)),
+            lambda: hop(5, fin.at[half], fin.at[half], p.at(p.s, one)),
         )
 
         def xy_sum(h):
@@ -487,7 +501,7 @@
             fin[half] = (zt[...].astype(F32) + zp[...].astype(F32)).astype(BF16)
             z_cps[2]().start()
         if stage == 6:
-            copy_to(fin.at[other], fin.at[other], send.at[k, 5], recv.at[k, 5], p.at(p.s, one)).wait_recv()
+            hop(5, fin.at[other], fin.at[other], p.at(p.s, one)).wait_recv()
             for cp in z_cps:
                 cp().wait_send()
             for cp in cps:
@@ -515,15 +529,16 @@
 
     def body(n, lo, first):
         a, dh = a_ref[...], dh_ref[...]
-        cut = pl.ds(lo, n)
-        g = dot(a, wg[:, cut])
-        u = dot(a, wu[:, cut])
-        da = dot_nt(dh, wd[cut, :]).astype(BF16).astype(F32)
-        sig, si = gated(g)
-        du = (da * si).astype(BF16)
-        dg = (da * u * (sig + si * (1.0 - sig))).astype(BF16)
+        for at, width in pieces_of(0, n):
+            cut = pl.ds(lo + at, width)
+            g = dot(a, wg[:, cut])
+            u = dot(a, wu[:, cut])
+            da = dot_nt(dh, wd[cut, :]).astype(BF16).astype(F32)
+            sig, si = gated(g)
+            dus[:, at : at + width] = (da * si).astype(BF16)
+            dgs[:, at : at + width] = (da * u * (sig + si * (1.0 - sig))).astype(BF16)
         at_tile = a_t[i]
-        pg, pu = dot(at_tile, dg), dot(at_tile, du)
+        pg, pu = dot(at_tile, dgs[:, :n]), dot(at_tile, dus[:, :n])
 
         @pl.when(i == 0)
         def _():
@@ -579,6 +594,7 @@
         + [pltpu.VMEM((2, 2, 2) + shape, BF16) for shape in BULK]
         + bufs
         + [pltpu.VMEM((D, FF), BF16), pltpu.VMEM((D, FF), BF16), pltpu.VMEM((FF, D), BF16)]
+        + [pltpu.VMEM((TILE, 512), BF16)] * 2
         + [pltpu.SemaphoreType.DMA((NP, 7)), pltpu.SemaphoreType.DMA((NP, 7)), pltpu.SemaphoreType.DMA((11,))],
         compiler_params=pltpu.CompilerParams(
             collective_id=1, has_side_effects=True, vmem_limit_bytes=VMEM_LIMIT, dimension_semantics=("arbitrary", "arbitrary")

time: 248 us -> 234 us (0.944)
  Pallas kernels: 240 us -> 226 us
    pallas_call x1, Pallas kernels: 91.6 us -> 82.9 us  [backward0(): pl.pallas_call(backward0_kernel, grid=(len(CHUNKS), TILES), out_shape=[up...]
    pallas_call x1, Pallas kernels: 88.3 us -> 83.3 us  [layer1(): pl.pallas_call(layer1_kernel, grid=(TILES,), out_shape=[jax.ShapeDtypeStr...]
where the time goes in v3:
time: 234 us
  Pallas kernels  226 us (97%)
  other arithmetic  6.75 us (3%)
    pallas_call x1, Pallas kernels, layer1(): pl.pallas_call(layer1_kernel, grid=(TILES,), out_shape=[jax.ShapeDtypeStr...  83.3 us
    pallas_call x1, Pallas kernels, backward0(): pl.pallas_call(backward0_kernel, grid=(len(CHUNKS), TILES), out_shape=[up...  82.9 us
    pallas_call x1, Pallas kernels, forward(): pl.pallas_call(forward_kernel, grid=(FORWARD_STEPS,), out_shape=[jax.Shap...  60 us
    convert_element_type x2, other arithmetic, adamw(): return ((w - 0.02 * step).astype(BF16), m, v)  6.75 us

profile of v3, /device:TPU:0, one launch (start us, length us, event | category | flops | bytes accessed | tf_op | source)
XLA Modules:
  0.0 233.8 jit_solution(12590114524669849824)
XLA Ops:
  0.6 60.0 %forward.1 = (bf16[4096,512]{1,0:T(8,128)(2,1)}, bf16[4096,1664]{1,0:T(8,128)(2,1)}, bf16[4096,512]{1,0:T(8,128)(2,1)}, bf16[8,64,1664]{2,1,0:T(8,128)(2,1)}, bf...) custom-call(bf16[2,64,1664]{2,1,0:T(8,128)(2,1)} %og.1, ...), custom_call_target="tpu_custom_call" | custom-call | tf_op jit(solution)/shard_map/forward/pallas_call | solution.py:227
  60.7 83.3 %layer1.1 = (bf16[4096,512]{1,0:T(8,128)(2,1)}, bf16[512,1664]{1,0:T(8,128)(2,1)}, bf16[512,1664]{1,0:T(8,128)(2,1)}, bf16[8,4,208,128]{3,2,1,0:T(8,128)(2,1)}, bf16[8,4,208,128]{3,2,1,0:T(8,128)(2,1)}) custom-call(bf16[4096,512]{1,0:T(8,128)(2,1)} %get-tuple-element.27.h_ref, bf16[4096,512]{1,0:T(8,128)(2,1)} %bitcast.12, ...), custom_call_target="tpu_custom_call" | custom-call | tf_op jit(solution)/shard_map/layer1/pallas_call | solution.py:298
  143.9 0.0 copy-start
  143.9 82.9 %backward0.1 = (bf16[2,64,1664]{2,1,0:T(8,128)(2,1)}, bf16[2,64,1664]{2,1,0:T(8,128)(2,1)}, bf16[2,208,512]{2,1,0:T(8,128)(2,1)}) custom-call(bf16[4096,512]{1,0:T(8,128)(2,1)} %get-tuple-element.26.refs_0_, bf16[4096,512]{1,0:T(8,128)(2,1)} %get-tuple-element.32.refs_1_, bf16[512,1664]{1,0:T(8,128)(2,1)} %bitcast.14, bf16[512,1664]{1,0:T(8,128)(2,1)} %bitcast.15, ...), custom_call_target="tpu_custom_call" | custom-call | tf_op jit(solution)/shard_map/backward0/pallas_call | solution.py:585
  226.9 0.0 copy-done
  226.9 0.0 copy-start.1
  226.9 0.0 copy-start.2
  226.9 0.0 copy-start.3
  226.9 0.0 copy-start.4
  226.9 0.0 copy-start.5
  226.9 0.0 copy-start.6
  226.9 0.0 copy-start.7
  226.9 3.3 %fusion.10 = (bf16[2,208,512]{2,1,0:T(8,128)(2,1)}, f32[2,208,512]{2,1,0:T(8,128)}, f32[2,208,512]{2,1,0:T(8,128)}) fusion(bf16[2,208,512]{2,1,0:T(8,128)(2,1)S(1)} %copy-done, bf16[2,208,512]{2,1,0:T(8,128)(2,1)} %get-tuple-element.42, f32[2,208,512]{2,1,0:T(8,128)} %param.21, f32[2,208,512]{2,1,0:T(8,128)} %param.18), kind=kLoop, calls=%fused_computation.22 | loop fusion | flops 3407872 | bytes 4685824 | tf_op jit(solution)/shard_map/convert_element_type | solution.py:610
  230.2 0.0 copy-done.1
  230.2 0.0 copy-done.2
  230.2 0.0 copy-done.3
  230.2 0.0 copy-done.4
  230.2 0.0 copy-done.5
  230.2 0.0 copy-done.6
  230.3 0.0 copy-done.7
  230.3 3.5 %fusion.2 = (bf16[2,64,1664]{2,1,0:T(8,128)(2,1)}, f32[2,64,1664]{2,1,0:T(8,128)}, f32[2,64,1664]{2,1,0:T(8,128)}, bf16[2,64,1664]{2,1,0:T(8,128)(2,1)}, f32[2,64,1664]{2,1,0:T(8,128)}, /*index=5*/f32[2,64,1664]{2,1,0:T(8,128)}) fusion(bf16[2,64,1664]{2,1,0:T(8,128)(2,1)S(1)} %copy-done.1, bf16[2,64,1664]{2,1,0:T(8,128)(2,1)S(1)} %copy-done.7, ...), kind=kLoop, calls=%fused_computation.14 | loop fusion | flops 6815744 | bytes 9371648 | tf_op jit(solution)/shard_map/convert_element_type | solution.py:610
Async XLA Ops:
  143.9 82.9 %copy-start = (bf16[2,208,512]{2,1,0:T(8,128)(2,1)S(1)}, bf16[2,208,512]{2,1,0:T(8,128)(2,1)}, u32[]{:S(2)}) copy-start(bf16[2,208,512]{2,1,0:T(8,128)(2,1)} %od.1) | copy-start | bytes 1277956
  226.9 3.4 %copy-start.1 = (bf16[2,64,1664]{2,1,0:T(8,128)(2,1)S(1)}, bf16[2,64,1664]{2,1,0:T(8,128)(2,1)}, u32[]{:S(2)}) copy-start(bf16[2,64,1664]{2,1,0:T(8,128)(2,1)} %og.1) | copy-start | bytes 1277956
  226.9 3.3 %copy-start.2 = (bf16[2,64,1664]{2,1,0:T(8,128)(2,1)S(1)}, bf16[2,64,1664]{2,1,0:T(8,128)(2,1)}, u32[]{:S(2)}) copy-start(bf16[2,64,1664]{2,1,0:T(8,128)(2,1)} %ou.1) | copy-start | bytes 1277956
  226.9 3.3 %copy-start.3 = (f32[2,64,1664]{2,1,0:T(8,128)S(1)}, f32[2,64,1664]{2,1,0:T(8,128)}, u32[]{:S(2)}) copy-start(f32[2,64,1664]{2,1,0:T(8,128)} %param.19) | copy-start | bytes 2555908
  226.9 3.3 %copy-start.4 = (f32[2,64,1664]{2,1,0:T(8,128)S(1)}, f32[2,64,1664]{2,1,0:T(8,128)}, u32[]{:S(2)}) copy-start(f32[2,64,1664]{2,1,0:T(8,128)} %param.16) | copy-start | bytes 2555908
  226.9 3.3 %copy-start.5 = (f32[2,64,1664]{2,1,0:T(8,128)S(1)}, f32[2,64,1664]{2,1,0:T(8,128)}, u32[]{:S(2)}) copy-start(f32[2,64,1664]{2,1,0:T(8,128)} %param.20) | copy-start | bytes 2555908
  226.9 3.3 %copy-start.6 = (f32[2,64,1664]{2,1,0:T(8,128)S(1)}, f32[2,64,1664]{2,1,0:T(8,128)}, u32[]{:S(2)}) copy-start(f32[2,64,1664]{2,1,0:T(8,128)} %param.17) | copy-start | bytes 2555908
  226.9 3.3 %copy-start.7 = (bf16[2,64,1664]{2,1,0:T(8,128)(2,1)S(1)}, bf16[2,64,1664]{2,1,0:T(8,128)(2,1)}, u32[]{:S(2)}) copy-start(bf16[2,64,1664]{2,1,0:T(8,128)(2,1)} %get-tuple-element.40) | copy-start | bytes 1277956

commit v4 on v3

--- a/solution.py
+++ b/solution.py
@@ -82,16 +82,17 @@
 FORWARD_STEPS = 3 * TILES
 OWN, PASS, DIAG, DONE = range(4)
 GATHER_PLAN = {
-    0: ((OWN, 0, 1), (PASS, 0, 1), (OWN, 2, 3), (DIAG, 0, 1), (DONE, 0, 1)),
-    2: ((PASS, 2, 3), (OWN, 4, 5)),
-    4: ((DIAG, 2, 3), (DONE, 2, 3)),
-    5: ((PASS, 4), (OWN, 6)),
-    6: ((PASS, 5), (OWN, 7)),
+    0: ((OWN, 0, 1, 2), (PASS, 0, 1), (OWN, 3), (DIAG, 0, 1), (DONE, 0, 1), (PASS, 2)),
+    1: ((PASS, 3), (OWN, 4, 5)),
+    4: ((DIAG, 2, 3), (DONE, 2, 3), (OWN, 6)),
+    5: ((PASS, 4), (OWN, 7)),
+    6: ((PASS, 5),),
+    7: ((PASS, 6),),
     8: ((DIAG, 4), (DONE, 4)),
-    9: ((PASS, 6),),
+    9: ((PASS, 7),),
     10: ((DIAG, 5),),
-    11: ((PASS, 7),),
-    12: ((DIAG, 6, 7), (DONE, 5, 6, 7)),
+    11: ((DIAG, 6),),
+    12: ((DIAG, 7), (DONE, 5, 6, 7)),
 }
 
 

time: 234 us -> 229 us (0.979)
  Pallas kernels: 226 us -> 222 us
    pallas_call x1, Pallas kernels: 60 us -> 55.9 us  [forward(): pl.pallas_call(forward_kernel, grid=(FORWARD_STEPS,), out_shape=[jax.Shap...]
where the time goes in v4:
time: 229 us
  Pallas kernels  222 us (97%)
  other arithmetic  6.75 us (3%)
    pallas_call x1, Pallas kernels, layer1(): pl.pallas_call(layer1_kernel, grid=(TILES,), out_shape=[jax.ShapeDtypeStr...  83.3 us
    pallas_call x1, Pallas kernels, backward0(): pl.pallas_call(backward0_kernel, grid=(len(CHUNKS), TILES), out_shape=[up...  82.5 us
    pallas_call x1, Pallas kernels, forward(): pl.pallas_call(forward_kernel, grid=(FORWARD_STEPS,), out_shape=[jax.Shap...  55.9 us
    convert_element_type x2, other arithmetic, adamw(): return ((w - 0.02 * step).astype(BF16), m, v)  6.75 us

profile of v4, /device:TPU:0, one launch (start us, length us, event | category | flops | bytes accessed | tf_op | source)
XLA Modules:
  0.0 229.2 jit_solution(12861524766176020883)
XLA Ops:
  0.6 55.9 %forward.1 = (bf16[4096,512]{1,0:T(8,128)(2,1)}, bf16[4096,1664]{1,0:T(8,128)(2,1)}, bf16[4096,512]{1,0:T(8,128)(2,1)}, bf16[8,64,1664]{2,1,0:T(8,128)(2,1)}, bf...) custom-call(bf16[2,64,1664]{2,1,0:T(8,128)(2,1)} %og.1, ...), custom_call_target="tpu_custom_call" | custom-call | tf_op jit(solution)/shard_map/forward/pallas_call | solution.py:228
  56.5 83.3 %layer1.1 = (bf16[4096,512]{1,0:T(8,128)(2,1)}, bf16[512,1664]{1,0:T(8,128)(2,1)}, bf16[512,1664]{1,0:T(8,128)(2,1)}, bf16[8,4,208,128]{3,2,1,0:T(8,128)(2,1)}, bf16[8,4,208,128]{3,2,1,0:T(8,128)(2,1)}) custom-call(bf16[4096,512]{1,0:T(8,128)(2,1)} %get-tuple-element.27.h_ref, bf16[4096,512]{1,0:T(8,128)(2,1)} %bitcast.12, ...), custom_call_target="tpu_custom_call" | custom-call | tf_op jit(solution)/shard_map/layer1/pallas_call | solution.py:299
  139.8 0.0 copy-start
  139.8 82.5 %backward0.1 = (bf16[2,64,1664]{2,1,0:T(8,128)(2,1)}, bf16[2,64,1664]{2,1,0:T(8,128)(2,1)}, bf16[2,208,512]{2,1,0:T(8,128)(2,1)}) custom-call(bf16[4096,512]{1,0:T(8,128)(2,1)} %get-tuple-element.26.refs_0_, bf16[4096,512]{1,0:T(8,128)(2,1)} %get-tuple-element.32.refs_1_, bf16[512,1664]{1,0:T(8,128)(2,1)} %bitcast.14, bf16[512,1664]{1,0:T(8,128)(2,1)} %bitcast.15, ...), custom_call_target="tpu_custom_call" | custom-call | tf_op jit(solution)/shard_map/backward0/pallas_call | solution.py:586
  222.3 0.0 copy-done
  222.3 0.0 copy-start.1
  222.3 0.0 copy-start.2
  222.3 0.0 copy-start.3
  222.3 0.0 copy-start.4
  222.4 0.0 copy-start.5
  222.4 0.0 copy-start.6
  222.4 0.0 copy-start.7
  222.4 3.3 %fusion.10 = (bf16[2,208,512]{2,1,0:T(8,128)(2,1)}, f32[2,208,512]{2,1,0:T(8,128)}, f32[2,208,512]{2,1,0:T(8,128)}) fusion(bf16[2,208,512]{2,1,0:T(8,128)(2,1)S(1)} %copy-done, bf16[2,208,512]{2,1,0:T(8,128)(2,1)} %get-tuple-element.42, f32[2,208,512]{2,1,0:T(8,128)} %param.21, f32[2,208,512]{2,1,0:T(8,128)} %param.18), kind=kLoop, calls=%fused_computation.22 | loop fusion | flops 3407872 | bytes 4685824 | tf_op jit(solution)/shard_map/convert_element_type | solution.py:611
  225.7 0.0 copy-done.1
  225.7 0.0 copy-done.2
  225.7 0.0 copy-done.3
  225.7 0.0 copy-done.4
  225.7 0.0 copy-done.5
  225.7 0.0 copy-done.6
  225.7 0.0 copy-done.7
  225.7 3.5 %fusion.2 = (bf16[2,64,1664]{2,1,0:T(8,128)(2,1)}, f32[2,64,1664]{2,1,0:T(8,128)}, f32[2,64,1664]{2,1,0:T(8,128)}, bf16[2,64,1664]{2,1,0:T(8,128)(2,1)}, f32[2,64,1664]{2,1,0:T(8,128)}, /*index=5*/f32[2,64,1664]{2,1,0:T(8,128)}) fusion(bf16[2,64,1664]{2,1,0:T(8,128)(2,1)S(1)} %copy-done.1, bf16[2,64,1664]{2,1,0:T(8,128)(2,1)S(1)} %copy-done.7, ...), kind=kLoop, calls=%fused_computation.14 | loop fusion | flops 6815744 | bytes 9371648 | tf_op jit(solution)/shard_map/convert_element_type | solution.py:611
Async XLA Ops:
  139.8 82.5 %copy-start = (bf16[2,208,512]{2,1,0:T(8,128)(2,1)S(1)}, bf16[2,208,512]{2,1,0:T(8,128)(2,1)}, u32[]{:S(2)}) copy-start(bf16[2,208,512]{2,1,0:T(8,128)(2,1)} %od.1) | copy-start | bytes 1277956
  222.3 3.4 %copy-start.1 = (bf16[2,64,1664]{2,1,0:T(8,128)(2,1)S(1)}, bf16[2,64,1664]{2,1,0:T(8,128)(2,1)}, u32[]{:S(2)}) copy-start(bf16[2,64,1664]{2,1,0:T(8,128)(2,1)} %og.1) | copy-start | bytes 1277956
  222.3 3.3 %copy-start.2 = (bf16[2,64,1664]{2,1,0:T(8,128)(2,1)S(1)}, bf16[2,64,1664]{2,1,0:T(8,128)(2,1)}, u32[]{:S(2)}) copy-start(bf16[2,64,1664]{2,1,0:T(8,128)(2,1)} %ou.1) | copy-start | bytes 1277956
  222.3 3.3 %copy-start.3 = (f32[2,64,1664]{2,1,0:T(8,128)S(1)}, f32[2,64,1664]{2,1,0:T(8,128)}, u32[]{:S(2)}) copy-start(f32[2,64,1664]{2,1,0:T(8,128)} %param.19) | copy-start | bytes 2555908
  222.3 3.3 %copy-start.4 = (f32[2,64,1664]{2,1,0:T(8,128)S(1)}, f32[2,64,1664]{2,1,0:T(8,128)}, u32[]{:S(2)}) copy-start(f32[2,64,1664]{2,1,0:T(8,128)} %param.16) | copy-start | bytes 2555908
  222.4 3.3 %copy-start.5 = (f32[2,64,1664]{2,1,0:T(8,128)S(1)}, f32[2,64,1664]{2,1,0:T(8,128)}, u32[]{:S(2)}) copy-start(f32[2,64,1664]{2,1,0:T(8,128)} %param.20) | copy-start | bytes 2555908
  222.4 3.3 %copy-start.6 = (f32[2,64,1664]{2,1,0:T(8,128)S(1)}, f32[2,64,1664]{2,1,0:T(8,128)}, u32[]{:S(2)}) copy-start(f32[2,64,1664]{2,1,0:T(8,128)} %param.17) | copy-start | bytes 2555908
  222.4 3.3 %copy-start.7 = (bf16[2,64,1664]{2,1,0:T(8,128)(2,1)S(1)}, bf16[2,64,1664]{2,1,0:T(8,128)(2,1)}, u32[]{:S(2)}) copy-start(bf16[2,64,1664]{2,1,0:T(8,128)(2,1)} %get-tuple-element.40) | copy-start | bytes 1277956
